TPU v7x, 256 devices: a whole 4x4x8 slice. The times are simulated.
256 devices in a mesh: slot: 8 (over z_hi, x), region: 32 (over z_lo, y, core).
Axes of the slice: x: 4, y: 4, z: 8 (z_hi: 2, z_lo: 4; z = z_hi * 4 + z_lo), core: 2. Of those that a mesh axis runs over, the one named last changes fastest.
Arguments:
- ensemble: bfloat16 [16, 256, 512, 128], P('slot', 'region'), may hold values from -6 to 6
- observations: float32 [16, 256, 1024], P('slot', 'region'), may hold values from -12 to 12
- operator_weight: bfloat16 [1024, 512], replicated, may hold values from -0.25 to 0.25
- obs_precision: float32 [1024], replicated, may hold values from 0.02 to 0.2
- channel_mask: int32 [16, 1024], P('slot'), may hold values 0 or 1
Outputs:
- analysis: bfloat16 [16, 256, 512, 128], P('slot', 'region')
All inputs are finite; a program needn't handle non-finite values. No bound on the sum of `channel_mask` on one device may be relied on, other than what follows from the above.
Results may differ from a plain program's by a relative error of at most 0.014.
Values may be sent and summed in bfloat16 or wider, within the bound.
A program may use at most 64 MiB of HBM per device.

v0:
```python
import jax
import jax.numpy as jnp
from jax import lax
from jax.sharding import PartitionSpec as P

OUTER = 2
NS_STEPS = 8


LOCAL_WEIGHT = 0.5


def extended(cells, sides, width):
    for axis, dim in sides:
        count = lax.axis_size(axis)
        head = lax.slice_in_dim(cells, 0, width, axis=dim)
        tail = lax.slice_in_dim(cells, cells.shape[dim] - width, cells.shape[dim], axis=dim)
        cells = jnp.concatenate(
            [
                lax.ppermute(tail, axis, [(i, (i + 1) % count) for i in range(count)]),
                cells,
                lax.ppermute(head, axis, [((i + 1) % count, i) for i in range(count)]),
            ],
            axis=dim,
        )
    return cells


def in_blocks(array, dim, count):
    dims = array.shape
    tiles = array.reshape(*dims[:dim], count, dims[dim] // count, *dims[dim + 1 :])
    return jnp.moveaxis(tiles, dim, 0)


def summed_on_arrival(array, axis, dim):
    count = lax.axis_size(axis)
    tiles = lax.all_to_all(in_blocks(array, dim, count), axis, 0, 0, tiled=True)
    return jnp.sum(tiles, axis=0)


def copy_for_each(array, axis):
    count = lax.axis_size(axis)
    return lax.all_to_all(
        jnp.broadcast_to(array[None], (count, *array.shape)), axis, 0, 0, tiled=True
    )


def laid_out(tiles, dim):
    dims = list(tiles.shape[1:])
    dims[dim] *= tiles.shape[0]
    return jnp.moveaxis(tiles, 0, dim).reshape(dims)


def gather_directly(array, axis, dim):
    tiles = copy_for_each(array, axis)
    return laid_out(tiles, dim)


def local_quads(misfit, weights):
    member_mean = jnp.mean(misfit.astype(jnp.float32), axis=-1)
    spread = (misfit.astype(jnp.float32) - member_mean[..., None]).astype(jnp.bfloat16)
    weighted = (weights[:, None, :, None] * spread.astype(jnp.float32)).astype(jnp.bfloat16)
    innovation = (-weights[:, None, :] * member_mean).astype(jnp.bfloat16)
    gram_part = jnp.einsum("spcm,spcn->pmn", weighted, spread, preferred_element_type=jnp.float32)
    grad_part = jnp.einsum("spcm,spc->pm", spread, innovation, preferred_element_type=jnp.float32)
    return jnp.concatenate([gram_part, grad_part[:, None, :]], axis=1)


def inverse_root(gram):
    members = gram.shape[-1]
    identity = jnp.eye(members, dtype=jnp.float32)
    shifted = gram + (members - 1.0) * identity
    norm_size = jnp.sqrt(jnp.sum(shifted * shifted, axis=(1, 2)))
    iterate = shifted / norm_size[:, None, None]
    factor = jnp.broadcast_to(identity, gram.shape)
    for number in range(NS_STEPS):
        middle = 1.5 * identity - 0.5 * jnp.einsum(
            "bij,bjk->bik", factor, iterate, precision=lax.Precision.HIGHEST
        )
        iterate = jnp.einsum("bij,bjk->bik", iterate, middle, precision=lax.Precision.HIGHEST)
        factor = jnp.einsum("bij,bjk->bik", middle, factor, precision=lax.Precision.HIGHEST)
    return factor / jnp.sqrt(norm_size)[:, None, None]


def transform(totals):
    members = totals.shape[-1]
    gram = totals[:, :members, :]
    grad = totals[:, members, :]
    inv_root = inverse_root(gram)
    inner = jnp.einsum("bij,bj->bi", inv_root, grad, precision=lax.Precision.HIGHEST)
    along = jnp.einsum("bij,bj->bi", inv_root, inner, precision=lax.Precision.HIGHEST)
    return (jnp.sqrt(members - 1.0) * inv_root + along[:, :, None]).astype(jnp.bfloat16)


def apply_mixing(states, mixing):
    centre = jnp.mean(states.astype(jnp.float32), axis=-1, keepdims=True)
    deviation = (states.astype(jnp.float32) - centre).astype(jnp.bfloat16)
    moved = jnp.einsum("sprm,pmn->sprn", deviation, mixing, preferred_element_type=jnp.float32)
    return (centre + moved).astype(jnp.bfloat16)


def shards(ensemble, observations, operator_weight, obs_precision, channel_mask):
    weights = obs_precision[None, :] * channel_mask.astype(jnp.float32) / OUTER
    states = ensemble
    for outer_step in range(OUTER):
        squashed = jnp.tanh(states.astype(jnp.float32)).astype(jnp.bfloat16)
        predicted = jnp.einsum(
            "cr,sprm->spcm", operator_weight, squashed, preferred_element_type=jnp.float32
        )
        misfit = (predicted - observations[..., None]).astype(jnp.bfloat16)
        quad_terms = local_quads(misfit, weights)
        widened = extended(quad_terms, (("region", 0),), 1)
        localized = quad_terms + LOCAL_WEIGHT * (widened[:-2] + widened[2:])
        shares = summed_on_arrival(localized, "slot", 0)
        mixing = gather_directly(transform(shares), "slot", 0)
        states = apply_mixing(states, mixing)
    return states


def solution(mesh):
    return jax.shard_map(
        shards,
        mesh=mesh,
        in_specs=(
            P("slot", "region", None, None),
            P("slot", "region", None),
            P(),
            P(),
            P("slot", None),
        ),
        out_specs=P("slot", "region", None, None),
        check_vma=False,
    )
```

profile of v0, /device:TPU:25, one launch (start us, length us, event | category | flops | bytes accessed | tf_op | source)
XLA Modules:
  0.0 137.0 jit_solution(2041063851630591672)
XLA Ops:
  0.0 3.0 %copy.18 = bf16[2,8,512,128]{2,3,0,1:T(8,128)(2,1)S(1)} copy(bf16[2,8,512,128]{3,2,1,0:T(8,128)(2,1)} %param.5) | data formatting | bytes 4194304 | tf_op args[0]
  3.0 1.1 fusion.4
  4.2 2.5 %bitcast_reduce_fusion.1 = (f32[2,8,1024]{2,1,0:T(8,128)S(1)}, bf16[2,8,128,1024]{3,2,1,0:T(8,128)(2,1)S(1)}) fusion(f32[2,8,1024]{2,1,0:T(8,128)S(1)} %copy-done.4, bf16[1024,512]{1,0:T(8,128)(2,1)S(1)} %copy-done, bf16[2,8,512,128]{2,3,0,1:T(8,128)(2,1)S(1)} %get-tuple-element.9), kind=kOutput, calls=%fused_computation.4 | convolution fusion | flops 2155855872 | bytes 7471104 | tf_op jit(solution)/shard_map/cr,sprm->spcm/dot_general | solution.py:107
  6.7 1.2 fusion.49
  7.9 1.8 %fusion.27 = f32[8,128,128]{2,1,0:T(8,128)S(1)} fusion(bf16[2,8,128,1024]{3,2,1,0:T(8,128)(2,1)S(1)} %get-tuple-element.20, f32[2,8,1024]{2,1,0:T(8,128)S(1)} %get-tuple-element.18, f32[2,1024]{1,0:T(2,128)S(1)} %get-tuple-element.6), kind=kOutput, calls=%fused_computation.35 | convolution fusion | flops 555745280 | bytes 4792320 | tf_op jit(solution)/shard_map/spcm,spcn->pmn/dot_general | solution.py:64
  9.7 1.9 %collective-permute-start = (f32[1,129,128]{2,1,0:T(8,128)S(1)}, f32[1,129,128]{2,1,0:T(8,128)S(1)}, u32[]{:S(2)}, u32[]{:S(2)}) collective-permute-start(f32[1,129,128]{2,1,0:T(8,128)S(1)} %get-tuple-element.13), channel_id=1, source_target_pairs={{0,1},{1,2},{2,3},{3,4},{4,5},{5,6},{6,7},{7,8},{8,9},{9,10},{10,1... | collective-permute-start | bytes 198152 | tf_op jit(solution)/shard_map/ppermute | solution.py:20
  11.6 1.4 collective-permute-done
  13.0 4.5 %collective-permute-done.1 = f32[1,129,128]{2,1,0:T(8,128)S(1)} collective-permute-done((f32[1,129,128]{2,1,0:T(8,128)S(1)}, f32[1,129,128]{2,1,0:T(8,128)S(1)}, u32[]{:S(2)}, u32[]{:S(2)}) %collective-permute-start.1) | collective-permute-done | bytes 66080 | tf_op jit(solution)/shard_map/ppermute | solution.py:22
  17.5 0.5 copy.22
  18.1 24.9 %all_to_all.20 = f32[8,1,129,128]{3,1,2,0:T(1,128)} all-to-all(f32[8,1,129,128]{3,1,2,0:T(1,128)S(1)} %copy.22), channel_id=1, replica_groups=mesh['slot'=8,'region'=32] {'slot'}, dimensions={0} | all-to-all | bytes 1056768 | tf_op jit(solution)/shard_map/all_to_all | solution.py:37
  43.0 1.4 %reduce_sum.78 = f32[129,128]{1,0:T(8,128)S(1)} reduce(f32[8,1,129,128]{3,1,2,0:T(1,128)} %all_to_all.20, f32[]{:T(128)} %constant.7.clone.1), dimensions={0,1}, to_apply=%region_2.0 | reduce | flops 115584 | bytes 594436 | tf_op jit(solution)/shard_map/reduce_sum | solution.py:38
  44.5 0.6 multiply_reduce_fusion.1
  50.8 0.2 convolution_bitcast_fusion.2
  51.3 0.7 broadcast_in_dim.9
  52.0 3.8 %all-to-all-start.1 = ((bf16[8,1,128,128]{2,3,1,0:T(8,128)(2,1)}), bf16[8,1,128,128]{2,3,1,0:T(8,128)(2,1)S(1)}, u32[]{:S(2)}, u32[]{:S(2)}) async-start(bf16[8,1,128,128]{2,3,1,0:T(8,128)(2,1)} %broadcast_in_dim.9), calls=%async_computation.1 | async-start | bytes 524288 | tf_op jit(solution)/shard_map/all_to_all | solution.py:43
  55.9 10.0 %all-to-all-done.1 = bf16[8,1,128,128]{2,3,1,0:T(8,128)(2,1)S(1)} async-done(((bf16[8,1,128,128]{2,3,1,0:T(8,128)(2,1)}), bf16[8,1,128,128]{2,3,1,0:T(8,128)(2,1)S(1)}, u32[]{:S(2)}, u32[]{:S(2)}) %all-to-all-start.1) | async-done | bytes 262176 | tf_op jit(solution)/shard_map/all_to_all | solution.py:43
  65.9 2.5 %fusion.6 = (bf16[2,8,512,128]{2,3,0,1:T(8,128)(2,1)S(1)}, f32[2,8,512]{2,0,1:T(2,128)S(1)}, bf16[2,8,512,128]{2,3,0,1:T(8,128)(2,1)}) fusion(bf16[2,8,512,128]{2,3,0,1:T(8,128)(2,1)S(1)} %copy.18, f32[2,8,512]{2,0,1:T(2,128)S(1)} %broadcast_multiply_fusion.3, bf16[8,1,128,128]{2,3,1,0:T(8,128)(2,1)S(1)} %all-to-all-done.1), kind=kOutput, calls=%fused_computation.20 | convolution fusion | flops 276815872 | bytes 6619136 | tf_op jit(solution)/shard_map/sprm,pmn->sprn/dot_general | solution.py:98
  68.4 2.5 %bitcast_reduce_fusion = (f32[2,8,1024]{2,1,0:T(8,128)S(1)}, bf16[2,8,128,1024]{3,2,1,0:T(8,128)(2,1)S(1)}) fusion(f32[2,8,1024]{2,1,0:T(8,128)S(1)} %copy-done.4, bf16[1024,512]{1,0:T(8,128)(2,1)S(1)} %copy-done, bf16[2,8,512,128]{2,3,0,1:T(8,128)(2,1)S(1)} %get-tuple-element.7), kind=kOutput, calls=%fused_computation.1 | convolution fusion | flops 2155855872 | bytes 7471104 | tf_op jit(solution)/shard_map/cr,sprm->spcm/dot_general | solution.py:107
  70.9 1.8 %fusion.24 = f32[8,128,128]{2,1,0:T(8,128)S(1)} fusion(bf16[2,8,128,1024]{3,2,1,0:T(8,128)(2,1)S(1)} %get-tuple-element.23, f32[2,8,1024]{2,1,0:T(8,128)S(1)} %get-tuple-element.16, f32[2,1024]{1,0:T(2,128)S(1)} %get-tuple-element.6), kind=kOutput, calls=%fused_computation.34 | convolution fusion | flops 555745280 | bytes 4792320 | tf_op jit(solution)/shard_map/spcm,spcn->pmn/dot_general | solution.py:64
  72.6 1.2 fusion.46
  73.8 6.4 %collective-permute-start.2 = (f32[1,129,128]{2,1,0:T(8,128)S(1)}, f32[1,129,128]{2,1,0:T(8,128)S(1)}, u32[]{:S(2)}, u32[]{:S(2)}) collective-permute-start(f32[1,129,128]{2,1,0:T(8,128)S(1)} %get-tuple-element.11), channel_id=1, source_target_pairs={{0,1},{1,2},{2,3},{3,4},{4,5},{5,6},{6,7},{7,8},{8,9},{9,10},{10,1... | collective-permute-start | bytes 198152 | tf_op jit(solution)/shard_map/ppermute | solution.py:20
  80.2 1.4 collective-permute-done.2
  81.6 7.3 %collective-permute-done.3 = f32[1,129,128]{2,1,0:T(8,128)S(1)} collective-permute-done((f32[1,129,128]{2,1,0:T(8,128)S(1)}, f32[1,129,128]{2,1,0:T(8,128)S(1)}, u32[]{:S(2)}, u32[]{:S(2)}) %collective-permute-start.3) | collective-permute-done | bytes 66080 | tf_op jit(solution)/shard_map/ppermute | solution.py:22
  89.0 0.5 copy.28
  89.6 16.1 %all_to_all.21 = f32[8,1,129,128]{3,1,2,0:T(1,128)} all-to-all(f32[8,1,129,128]{3,1,2,0:T(1,128)S(1)} %copy.28), channel_id=1, replica_groups=mesh['slot'=8,'region'=32] {'slot'}, dimensions={0} | all-to-all | bytes 1056768 | tf_op jit(solution)/shard_map/all_to_all | solution.py:37
  105.6 1.4 %reduce_sum.83 = f32[129,128]{1,0:T(8,128)S(1)} reduce(f32[8,1,129,128]{3,1,2,0:T(1,128)} %all_to_all.21, f32[]{:T(128)} %constant.7.clone.1), dimensions={0,1}, to_apply=%region_6.0 | reduce | flops 115584 | bytes 594436 | tf_op jit(solution)/shard_map/reduce_sum | solution.py:38
  107.1 0.7 multiply_reduce_fusion
  114.0 0.7 broadcast_in_dim.11
  114.8 6.3 %all-to-all-start.3 = ((bf16[8,1,128,128]{2,3,1,0:T(8,128)(2,1)}), bf16[8,1,128,128]{2,3,1,0:T(8,128)(2,1)S(1)}, u32[]{:S(2)}, u32[]{:S(2)}) async-start(bf16[8,1,128,128]{2,3,1,0:T(8,128)(2,1)} %broadcast_in_dim.11), calls=%async_computation.3 | async-start | bytes 524288 | tf_op jit(solution)/shard_map/all_to_all | solution.py:43
  121.1 10.0 %all-to-all-done.3 = bf16[8,1,128,128]{2,3,1,0:T(8,128)(2,1)S(1)} async-done(((bf16[8,1,128,128]{2,3,1,0:T(8,128)(2,1)}), bf16[8,1,128,128]{2,3,1,0:T(8,128)(2,1)S(1)}, u32[]{:S(2)}, u32[]{:S(2)}) %all-to-all-start.3) | async-done | bytes 262176 | tf_op jit(solution)/shard_map/all_to_all | solution.py:43
  131.0 2.1 %fusion.8 = bf16[2,8,512,128]{2,3,0,1:T(8,128)(2,1)} fusion(bf16[2,8,512,128]{2,3,0,1:T(8,128)(2,1)S(1)} %copy-done.1, f32[2,8,512]{2,0,1:T(2,128)S(1)} %broadcast_multiply_fusion.2, bf16[8,1,128,128]{2,3,1,0:T(8,128)(2,1)S(1)} %all-to-all-done.3), kind=kOutput, calls=%fused_computation.23 | convolution fusion | flops 273678336 | bytes 4489216 | tf_op jit(solution)/shard_map/sprm,pmn->sprn/dot_general | solution.py:98
  133.1 3.9 %copy.31 = bf16[2,8,512,128]{3,2,1,0:T(8,128)(2,1)} copy(bf16[2,8,512,128]{2,3,0,1:T(8,128)(2,1)} %fusion.8) | data formatting | bytes 4194304 | tf_op jit(solution)/shard_map/convert_element_type | solution.py:99
  (74 shorter events, 10.6 us)
Async XLA Ops:
  0.0 4.2 %copy-start = (bf16[1024,512]{1,0:T(8,128)(2,1)S(1)}, bf16[1024,512]{1,0:T(8,128)(2,1)}, u32[]{:S(2)}) copy-start(bf16[1024,512]{1,0:T(8,128)(2,1)} %param.7) | copy-start | bytes 3145732
  0.0 4.1 %copy-start.2 = (s32[2,1024]{1,0:T(2,128)S(1)}, s32[2,1024]{1,0:T(2,128)}, u32[]{:S(2)}) copy-start(s32[2,1024]{1,0:T(2,128)} %param.9) | copy-start | bytes 24580
  0.0 4.1 %copy-start.3 = (f32[1024]{0:T(1024)S(1)}, f32[1024]{0:T(1024)}, u32[]{:S(2)}) copy-start(f32[1024]{0:T(1024)} %param.8) | copy-start | bytes 12292
  0.0 4.2 %copy-start.4 = (f32[2,8,1024]{2,1,0:T(8,128)S(1)}, f32[2,8,1024]{2,1,0:T(8,128)}, u32[]{:S(2)}) copy-start(f32[2,8,1024]{2,1,0:T(8,128)} %param.6) | copy-start | bytes 196612
  9.7 3.3 %collective-permute-start = (f32[1,129,128]{2,1,0:T(8,128)S(1)}, f32[1,129,128]{2,1,0:T(8,128)S(1)}, u32[]{:S(2)}, u32[]{:S(2)}) collective-permute-start(f32[1,129,128]{2,1,0:T(8,128)S(1)} %get-tuple-element.13), channel_id=1, source_target_pairs={{0,1},{1,2},{2,3},{3,4},{4,5},{5,6},{6,7},{7,8},{8,9},{9,10},{10,1... | collective-permute-start | bytes 198152 | tf_op jit(solution)/shard_map/ppermute | solution.py:20
  11.6 5.8 %collective-permute-start.1 = (f32[1,129,128]{2,1,0:T(8,128)S(1)}, f32[1,129,128]{2,1,0:T(8,128)S(1)}, u32[]{:S(2)}, u32[]{:S(2)}) collective-permute-start(f32[1,129,128]{2,1,0:T(8,128)S(1)} %get-tuple-element.14), channel_id=1, source_target_pairs={{1,0},{2,1},{3,2},{4,3},{5,4},{6,5},{7,6},{8,7},{9,8},{10,9},{11,1... | collective-permute-start | bytes 198152 | tf_op jit(solution)/shard_map/ppermute | solution.py:22
  52.0 13.8 %all-to-all-start.1 = ((bf16[8,1,128,128]{2,3,1,0:T(8,128)(2,1)}), bf16[8,1,128,128]{2,3,1,0:T(8,128)(2,1)S(1)}, u32[]{:S(2)}, u32[]{:S(2)}) async-start(bf16[8,1,128,128]{2,3,1,0:T(8,128)(2,1)} %broadcast_in_dim.9), calls=%async_computation.1 | async-start | bytes 524288 | tf_op jit(solution)/shard_map/all_to_all | solution.py:43
  73.8 7.8 %collective-permute-start.2 = (f32[1,129,128]{2,1,0:T(8,128)S(1)}, f32[1,129,128]{2,1,0:T(8,128)S(1)}, u32[]{:S(2)}, u32[]{:S(2)}) collective-permute-start(f32[1,129,128]{2,1,0:T(8,128)S(1)} %get-tuple-element.11), channel_id=1, source_target_pairs={{0,1},{1,2},{2,3},{3,4},{4,5},{5,6},{6,7},{7,8},{8,9},{9,10},{10,1... | collective-permute-start | bytes 198152 | tf_op jit(solution)/shard_map/ppermute | solution.py:20
  80.2 8.7 %collective-permute-start.3 = (f32[1,129,128]{2,1,0:T(8,128)S(1)}, f32[1,129,128]{2,1,0:T(8,128)S(1)}, u32[]{:S(2)}, u32[]{:S(2)}) collective-permute-start(f32[1,129,128]{2,1,0:T(8,128)S(1)} %get-tuple-element.12), channel_id=1, source_target_pairs={{1,0},{2,1},{3,2},{4,3},{5,4},{6,5},{7,6},{8,7},{9,8},{10,9},{11,1... | collective-permute-start | bytes 198152 | tf_op jit(solution)/shard_map/ppermute | solution.py:22
  89.0 42.0 %copy-start.1 = (bf16[2,8,512,128]{2,3,0,1:T(8,128)(2,1)S(1)}, bf16[2,8,512,128]{2,3,0,1:T(8,128)(2,1)}, u32[]{:S(2)}) copy-start(bf16[2,8,512,128]{2,3,0,1:T(8,128)(2,1)} %get-tuple-element.21) | copy-start | bytes 6291460
  114.8 16.2 %all-to-all-start.3 = ((bf16[8,1,128,128]{2,3,1,0:T(8,128)(2,1)}), bf16[8,1,128,128]{2,3,1,0:T(8,128)(2,1)S(1)}, u32[]{:S(2)}, u32[]{:S(2)}) async-start(bf16[8,1,128,128]{2,3,1,0:T(8,128)(2,1)} %broadcast_in_dim.11), calls=%async_computation.3 | async-start | bytes 524288 | tf_op jit(solution)/shard_map/all_to_all | solution.py:43
where the time goes:
time: 138 us; the launch traced here: 137 us
  blocking collectives  41 us (30%)
  waiting for transfers between devices  34.4 us (25%)
  matrix products  25.5 us (18%)
  starting transfers between devices  18.4 us (13%)
  local copies, waits for them, and re-layouts  9.69 us (7%)
  other arithmetic  5.8 us (4%)
  between operations  2.08 us (2%)
    all_to_all x2, blocking collectives, summed_on_arrival(): tiles = lax.all_to_all(in_blocks(array, dim, count), axis, 0, 0, tiled=True)  41 us
    all_to_all x2, waiting for transfers between devices, copy_for_each(): lax.all_to_all(jnp.broadcast_to(array[None], (count, *array.shape)), axis...  19.9 us
    ppermute x2, waiting for transfers between devices, extended(): lax.ppermute(head, axis, [((i + 1) % count, i) for i in range(count)])  11.8 us
    all_to_all x2, starting transfers between devices, copy_for_each(): lax.all_to_all(jnp.broadcast_to(array[None], (count, *array.shape)), axis...  10.1 us
    ppermute x2, starting transfers between devices, extended(): lax.ppermute(tail, axis, [(i, (i + 1) % count) for i in range(count)])  8.33 us
    dot_general x2, matrix products, shards(): jnp.einsum('cr,sprm->spcm', operator_weight, squashed, preferred_element_...  4.91 us
    dot_general x2, matrix products, apply_mixing(): jnp.einsum('sprm,pmn->sprn', deviation, mixing, preferred_element_type=jn...  4.59 us
    convert_element_type x1, local copies, waits for them, and re-layouts, apply_mixing(): return (centre + moved).astype(jnp.bfloat16)  3.91 us
  transfers between devices with their start and end apart: 6, of which 6 were waited for; matrix products, arithmetic and copies ran while one was open for 0% of the time, Pallas kernels for 0%

commit v1 on v0

v1 whole, which is shorter than its diff:
```python
import functools
import math

import jax
import jax.numpy as jnp
from jax import lax
from jax.experimental import pallas as pl
from jax.experimental.pallas import tpu as pltpu
from jax.sharding import PartitionSpec as P

OUTER = 2
NS_STEPS = 8
LOCAL_WEIGHT = 0.5
XN = 4

F32 = jnp.float32
BF16 = jnp.bfloat16
MESH = pl.DeviceIdType.MESH
NT = (((1,), (1,)), ((), ()))


def iota(shape, dim):
    return lax.broadcasted_iota(jnp.int32, shape, dim)


def halves(a):
    high = a.astype(BF16)
    return high, (a - high.astype(F32)).astype(BF16)


def product(a, b):
    (ah, al), (bh, bl) = a, b
    return (
        jnp.dot(ah, bl, preferred_element_type=F32)
        + jnp.dot(al, bh, preferred_element_type=F32)
        + jnp.dot(ah, bh, preferred_element_type=F32)
    )


def packed(gram):
    top, bottom = gram[0:64], gram[64:128]
    row, col = iota((64, 128), 0), iota((64, 128), 1)
    body = jnp.where(col >= row, top, pltpu.roll(bottom, 64, 1))
    diag = jnp.sum(jnp.where(col == row + 64, bottom, 0.0), axis=0, keepdims=True)
    tail_row = iota((16, 128), 0)
    grad = gram[128:129] + gram[129:130]
    tail = jnp.where(tail_row == 0, diag, jnp.where(tail_row == 1, grad, 0.0))
    return jnp.concatenate([body, tail], axis=0)


def message(pack):
    tail = pack[64:80]
    row = iota((16, 128), 0)
    grad = tail[1:2] + tail[2:3]
    high = grad.astype(BF16).astype(F32)
    tail = jnp.where(
        row == 0, tail, jnp.where(row == 1, high, jnp.where(row == 2, grad - high, 0.0))
    )
    return jnp.concatenate([pack[0:64].astype(BF16), tail.astype(BF16)], axis=0)


def unpacked(pack):
    top = pack[0:64]
    row, col = iota((64, 128), 0), iota((64, 128), 1)
    upper = jnp.where(col >= row, top, 0.0)
    lower = pltpu.roll(jnp.where(col < row, top, 0.0), 64, 1)
    lower = jnp.where(col == row + 64, pack[64:65], lower)
    half = jnp.concatenate([upper, lower], axis=0)
    row, col = iota((128, 128), 0), iota((128, 128), 1)
    return jnp.where(row == col, half, half + half.T), pack[65:66] + pack[66:67]


def transforms(packs):
    members = 128
    row, col = iota((128, 128), 0), iota((128, 128), 1)
    identity = jnp.where(row == col, 1.0, 0.0).astype(F32)
    grads, scales, iterates, factors = [], [], [], []
    for pack in packs:
        gram, grad = unpacked(pack)
        shifted = gram + (members - 1.0) * identity
        total = jnp.sum(jnp.sum(shifted * shifted, axis=0, keepdims=True), axis=1, keepdims=True)
        norm = jnp.sqrt(total)
        grads.append(grad)
        scales.append(1.0 / jnp.sqrt(norm))
        iterates.append(shifted * (1.0 / norm))
    count = len(packs)
    middles = [1.5 * identity - 0.5 * it for it in iterates]
    split_mid = [halves(m) for m in middles]
    factors = middles
    iterates = [product(halves(iterates[i]), split_mid[i]) for i in range(count)]
    for number in range(1, NS_STEPS):
        split_fac = [halves(f) for f in factors]
        split_it = [halves(it) for it in iterates]
        middles = [
            1.5 * identity - 0.5 * product(split_fac[i], split_it[i]) for i in range(count)
        ]
        split_mid = [halves(m) for m in middles]
        if number + 1 < NS_STEPS:
            iterates = [product(split_it[i], split_mid[i]) for i in range(count)]
        factors = [product(split_mid[i], split_fac[i]) for i in range(count)]
    out = []
    for i in range(count):
        root = factors[i] * scales[i]
        split_root = halves(root)
        grad = jnp.broadcast_to(grads[i], (16, 128))
        inner = product(halves(grad), split_root)
        along = product(halves(inner), split_root)
        out.append((math.sqrt(members - 1.0) * root + along[0:1]).astype(BF16))
    return out


def kernel(
    regions,
    x_hbm, obs_hbm, op_hbm, wt_hbm,
    x1_hbm, mix_out,
    xin, obs, op, wt, opw, amat, bvec,
    sq, sc, dev, cen, zb, pk, x1t, x1v,
    halo_out, halo_in, part, rs_in, z_out, z_in, mixbuf,
    load_sem, store_sem, halo_s, halo_r, rs_s, rs_r, z_s, z_r, ag_s, ag_r,
):
    slot, region = lax.axis_index("slot"), lax.axis_index("region")
    xi, zi = lax.rem(slot, XN), lax.div(slot, XN)
    z_peer = lax.rem(slot + XN, 2 * XN)
    before, after = lax.rem(region + regions - 1, regions), lax.rem(region + 1, regions)

    def x_peer(d):
        return zi * XN + lax.rem(xi + d, XN)

    barrier = pltpu.get_barrier_semaphore()
    for peer in [(x_peer(1), region), (x_peer(2), region), (x_peer(3), region),
                 (z_peer, region), (slot, before), (slot, after)]:
        pl.semaphore_signal(barrier, inc=1, device_id=peer, device_id_type=MESH)

    loads = [
        pltpu.make_async_copy(op_hbm, op, load_sem.at[0]),
        pltpu.make_async_copy(wt_hbm, wt, load_sem.at[1]),
        pltpu.make_async_copy(obs_hbm, obs, load_sem.at[2]),
        pltpu.make_async_copy(x_hbm.at[:, 0:1], xin.at[:, 0:1], load_sem.at[3]),
        pltpu.make_async_copy(x_hbm.at[:, 7:8], xin.at[:, 1:2], load_sem.at[4]),
        pltpu.make_async_copy(x_hbm.at[:, 1:7], xin.at[:, 2:8], load_sem.at[5]),
    ]
    for load in loads:
        load.start()
    for load in loads[:3]:
        load.wait()

    @pl.loop(0, 8)
    def _(ci):
        c = pl.multiple_of(ci * 128, 128)
        weight = [wt[t:t + 1, pl.ds(c, 128)] for t in range(2)]
        for ri in range(4):
            block = op[pl.ds(c, 128), ri * 128:(ri + 1) * 128].astype(F32).T
            for t in range(2):
                opw[t, ri * 128:(ri + 1) * 128, pl.ds(c, 128)] = (block * weight[t]).astype(BF16)

    for t in range(2):
        high, low = halves(obs[t] * wt[t:t + 1, :])
        both = jnp.dot(jnp.concatenate([high, low], axis=0), op[...], preferred_element_type=F32)
        for p in range(8):
            bvec[t, p] = both[p:p + 1] + both[p + 8:p + 9]

    for load in loads[3:]:
        load.wait()

    def squash(block, t, q, column):
        squashed = jnp.tanh(block).astype(BF16)
        wide = squashed.astype(F32)
        mean = jnp.sum(wide, axis=0, keepdims=True) * (1.0 / 128)
        sq[t, pl.ds(pl.multiple_of(q * 128, 128), 128), column * 128:(column + 1) * 128] = squashed
        at = t * 512 + column * 128
        sc[q, :, at:at + 128] = (wide - mean).astype(BF16)

    @pl.loop(0, 4)
    def _(step):
        t, part_row = lax.div(step, 2), pl.multiple_of(lax.rem(step, 2) * 256, 256)
        amat[t, pl.ds(part_row, 256), :] = jnp.dot(
            opw[t, pl.ds(part_row, 256), :], op[...], preferred_element_type=F32
        ).astype(BF16)
        for i in range(2):
            q = 2 * step + i
            for s in range(2):
                for column in range(4):
                    block = xin[s, q, column * 128:(column + 1) * 128, :].astype(F32).T
                    centre = jnp.sum(block, axis=0, keepdims=True) * (1.0 / 128)
                    at = s * 512 + column * 128
                    cen[q, :, at:at + 128] = centre
                    dev[q, :, at:at + 128] = (block - centre).astype(BF16)
                    squash(block, s, q, column)

    def position(p):
        return 0 if p == 0 else 1 if p == 7 else p + 1

    def halo_copies(k):
        return [
            pltpu.make_async_remote_copy(
                src_ref=halo_out.at[k, side], dst_ref=halo_in.at[k, 1 - side],
                send_sem=halo_s.at[k, side], recv_sem=halo_r.at[k, 1 - side],
                device_id=(slot, before if side == 0 else after), device_id_type=MESH,
            )
            for side in range(2)
        ]

    def halo_arrival(k, side):
        return pltpu.make_async_remote_copy(
            src_ref=halo_out.at[k, 1 - side], dst_ref=halo_in.at[k, side],
            send_sem=halo_s.at[k, 1 - side], recv_sem=halo_r.at[k, side],
            device_id=(slot, before if side == 0 else after), device_id_type=MESH,
        )

    def rs_copy(k, j):
        d = lax.rem(j - xi + XN, XN)
        return pltpu.make_async_remote_copy(
            src_ref=part.at[k, j], dst_ref=rs_in.at[k, d - 1],
            send_sem=rs_s.at[k, d - 1], recv_sem=rs_r.at[k, d - 1],
            device_id=(zi * XN + j, region), device_id_type=MESH,
        )

    def localize(k, j):
        for i in range(2):
            p = 2 * j + i
            left = halo_in[k, 0].astype(F32) if p == 0 else pk[position(p - 1)]
            right = halo_in[k, 1].astype(F32) if p == 7 else pk[position(p + 1)]
            part[k, j, i] = message(pk[position(p)] + LOCAL_WEIGHT * (left + right))

        @pl.when(xi != j)
        def _():
            rs_copy(k, j).start()

    def z_copy(k):
        return pltpu.make_async_remote_copy(
            src_ref=z_out.at[k], dst_ref=z_in.at[k], send_sem=z_s.at[k], recv_sem=z_r.at[k],
            device_id=(z_peer, region), device_id_type=MESH,
        )

    def ag_copy(k, d):
        own = pl.ds(2 * xi, 2)
        return pltpu.make_async_remote_copy(
            src_ref=mixbuf.at[k, own], dst_ref=mixbuf.at[k, own],
            send_sem=ag_s.at[k, d - 1], recv_sem=ag_r.at[k, d - 1],
            device_id=(x_peer(d), region), device_id_type=MESH,
        )

    def store(t, q):
        p = 0 if q == 0 else 7 if q == 1 else q - 1
        return pltpu.make_async_copy(x1v.at[t, q], x1_hbm.at[t, p], store_sem.at[t, q])

    for k in range(OUTER):
        @pl.loop(0, 4)
        def _(g):
            p0 = jnp.where(g == 0, 0, 2 * g - 1)
            p1 = jnp.where(g == 0, 7, 2 * g)
            if k > 0:
                for i, p in enumerate((p0, p1)):
                    q = 2 * g + i
                    moved = jnp.dot(mixbuf[k - 1, p], dev[q], preferred_element_type=F32)
                    for t in range(2):
                        for column in range(4):
                            at = t * 512 + column * 128
                            rounded = (cen[q, :, at:at + 128] + moved[:, at:at + 128]).astype(BF16)
                            x1t[q, :, at:at + 128] = rounded
                            squash(rounded.astype(F32), t, q, column)
            for t in range(2):
                lines = pl.ds(pl.multiple_of(g * 256, 256), 256)
                for n in range(2):
                    cols = slice(n * 256, (n + 1) * 256)
                    applied = jnp.dot(sq[t, lines, :], amat[t, :, cols], preferred_element_type=F32)
                    for i, p in enumerate((p0, p1)):
                        z = applied[i * 128:(i + 1) * 128]
                        mean = jnp.sum(z, axis=0, keepdims=True) * (1.0 / 128)
                        at = t * 512 + n * 256
                        zb[i, 0:128, at:at + 256] = (z - mean).astype(BF16)
                        pull = bvec[t, p, :, cols] - mean
                        high = pull.astype(BF16).astype(F32)
                        row = iota((16, 256), 0)
                        tail = jnp.where(row == 0, high, jnp.where(row == 1, pull - high, 0.0))
                        zb[i, 128:144, at:at + 256] = tail.astype(BF16)
            for i in range(2):
                q = 2 * g + i
                gram = lax.dot_general(zb[i], sc[q], NT, preferred_element_type=F32)
                pk[q] = packed(gram)

            @pl.when(g == 0)
            def _():
                for side in range(2):
                    halo_out[k, side] = message(pk[side])
                if k == 0:
                    pl.semaphore_wait(barrier, 6)
                for copy in halo_copies(k):
                    copy.start()

            @pl.when(g == 2)
            def _():
                localize(k, 1)

        localize(k, 2)
        halo_arrival(k, 0).wait_recv()
        localize(k, 0)
        halo_arrival(k, 1).wait_recv()
        localize(k, 3)

        if k == OUTER - 1:
            @pl.loop(0, 8)
            def _(q):
                for t in range(2):
                    for column in range(4):
                        at = t * 512 + column * 128
                        block = x1t[q, :, at:at + 128].astype(F32).T
                        x1v[t, q, column * 128:(column + 1) * 128, :] = block.astype(BF16)
            for t in range(2):
                for q in range(8):
                    store(t, q).start()

        for d in range(1, XN):
            pltpu.make_async_remote_copy(
                src_ref=part.at[k, 0], dst_ref=rs_in.at[k, d - 1],
                send_sem=rs_s.at[k, d - 1], recv_sem=rs_r.at[k, d - 1],
                device_id=(x_peer(d), region), device_id_type=MESH,
            ).wait_recv()
        sums = []
        for i in range(2):
            total = part[k, xi, i].astype(F32)
            for d in range(1, XN):
                total = total + rs_in[k, d - 1, i].astype(F32)
            sums.append(total)
            z_out[k, i] = message(total)
        z_copy(k).start()
        z_copy(k).wait_recv()
        mixes = transforms([sums[i] + z_in[k, i].astype(F32) for i in range(2)])
        for i in range(2):
            mixbuf[k, 2 * xi + i] = mixes[i]
        for d in range(1, XN):
            ag_copy(k, d).start()
        for d in range(1, XN):
            pltpu.make_async_remote_copy(
                src_ref=mixbuf.at[k, pl.ds(2 * xi, 2)],
                dst_ref=mixbuf.at[k, pl.ds(2 * lax.rem(xi + XN - d, XN), 2)],
                send_sem=ag_s.at[k, d - 1], recv_sem=ag_r.at[k, d - 1],
                device_id=(x_peer(d), region), device_id_type=MESH,
            ).wait_recv()

    mix_out[...] = mixbuf[OUTER - 1]
    for k in range(OUTER):
        for copy in halo_copies(k):
            copy.wait_send()
        for d in range(1, XN):
            pltpu.make_async_remote_copy(
                src_ref=part.at[k, 0], dst_ref=rs_in.at[k, d - 1],
                send_sem=rs_s.at[k, d - 1], recv_sem=rs_r.at[k, d - 1],
                device_id=(x_peer(d), region), device_id_type=MESH,
            ).wait_send()
            ag_copy(k, d).wait_send()
        z_copy(k).wait_send()
    for t in range(2):
        for q in range(8):
            store(t, q).wait()


def last_apply(x_ref, mix_ref, out_ref):
    mix = mix_ref[0].astype(F32)
    full = mix + (1.0 - jnp.sum(mix, axis=1, keepdims=True)) * (1.0 / 128)
    high, low = halves(full)
    for t in range(2):
        x = x_ref[t, 0]
        moved = lax.dot_general(x, low, NT, preferred_element_type=F32) + lax.dot_general(
            x, high, NT, preferred_element_type=F32
        )
        out_ref[t, 0] = moved.astype(BF16)


def shards(regions, ensemble, observations, operator_weight, obs_precision, channel_mask):
    weights = obs_precision[None, :] * channel_mask.astype(F32) / OUTER
    slots, patches, rows, members = ensemble.shape
    channels = operator_weight.shape[0]
    anywhere = pl.BlockSpec(memory_space=pl.ANY)
    dma, vmem = pltpu.SemaphoreType.DMA, pltpu.VMEM
    states, mixing = pl.pallas_call(
        functools.partial(kernel, regions),
        out_shape=(
            jax.ShapeDtypeStruct(ensemble.shape, BF16),
            jax.ShapeDtypeStruct((patches, members, members), BF16),
        ),
        in_specs=[anywhere] * 4,
        out_specs=(anywhere, pl.BlockSpec(memory_space=pltpu.VMEM)),
        scratch_shapes=[
            vmem((2, 8, 512, 128), BF16),
            vmem((2, 8, 1024), F32),
            vmem((1024, 512), BF16),
            vmem((2, 1024), F32),
            vmem((2, 512, 1024), BF16),
            vmem((2, 512, 512), BF16),
            vmem((2, 8, 1, 512), F32),
            vmem((2, 1024, 512), BF16),
            vmem((8, 128, 1024), BF16),
            vmem((8, 128, 1024), BF16),
            vmem((8, 1, 1024), F32),
            vmem((2, 144, 1024), BF16),
            vmem((8, 80, 128), F32),
            vmem((8, 128, 1024), BF16),
            vmem((2, 8, 512, 128), BF16),
            vmem((2, 2, 80, 128), BF16),
            vmem((2, 2, 80, 128), BF16),
            vmem((2, XN, 2, 80, 128), BF16),
            vmem((2, XN - 1, 2, 80, 128), BF16),
            vmem((2, 2, 80, 128), BF16),
            vmem((2, 2, 80, 128), BF16),
            vmem((2, 8, 128, 128), BF16),
            dma((6,)), dma((2, 8)),
            dma((2, 2)), dma((2, 2)),
            dma((2, XN - 1)), dma((2, XN - 1)),
            dma((2,)), dma((2,)),
            dma((2, XN - 1)), dma((2, XN - 1)),
        ],
        compiler_params=pltpu.CompilerParams(
            collective_id=0, has_side_effects=True, vmem_limit_bytes=40 << 20
        ),
        name="smoother",
    )(ensemble, observations, operator_weight, weights)
    block = pl.BlockSpec((2, 1, rows, members), lambda p: (0, p, 0, 0))
    return pl.pallas_call(
        last_apply,
        grid=(patches,),
        out_shape=jax.ShapeDtypeStruct(ensemble.shape, BF16),
        in_specs=[block, pl.BlockSpec((1, members, members), lambda p: (p, 0, 0))],
        out_specs=block,
        name="last_apply",
    )(states, mixing)


def solution(mesh):
    return jax.shard_map(
        functools.partial(shards, mesh.shape["region"]),
        mesh=mesh,
        in_specs=(
            P("slot", "region", None, None),
            P("slot", "region", None),
            P(),
            P(),
            P("slot", None),
        ),
        out_specs=P("slot", "region", None, None),
        check_vma=False,
    )
```

time: 138 us -> 68.2 us (0.49)
  the two profiles are of different devices: /device:TPU:25 before, /device:TPU:6 now
where the time goes in v1:
time: 68.2 us; the launch traced here: 67 us
  Pallas kernels  60.5 us (89%)
  local copies, waits for them, and re-layouts  5.69 us (8%)
  other arithmetic  0.71 us (1%)
    pallas_call x1, Pallas kernels, shards(): pl.pallas_call(functools.partial(kernel, regions), out_shape=(jax.ShapeDt...  53.5 us
    pallas_call x1, Pallas kernels, shards(): pl.pallas_call(last_apply, grid=(patches,), out_shape=jax.ShapeDtypeStruc...  7.01 us
    unnamed x10, local copies, waits for them, and re-layouts  5.69 us

profile of v1, /device:TPU:6, one launch (start us, length us, event | category | flops | bytes accessed | tf_op | source)
XLA Modules:
  0.0 67.0 jit_solution(2649297362451306523)
XLA Ops:
  0.0 0.7 %multiply_multiply_fusion.wt_hbm = f32[2,1024]{1,0:T(2,128)S(1)} fusion(s32[2,1024]{1,0:T(2,128)} %param.9, f32[1024]{0:T(1024)} %param.8), kind=kLoop, calls=%fused_computation | loop fusion | flops 6144 | bytes 20480 | tf_op jit(solution)/shard_map/div | solution.py:371
  0.7 0.0 copy-start
  0.7 1.6 %copy-done = bf16[2,8,512,128]{3,2,1,0:T(8,128)(2,1)S(1)} copy-done((bf16[2,8,512,128]{3,2,1,0:T(8,128)(2,1)S(1)}, bf16[2,8,512,128]{3,2,1,0:T(8,128)(2,1)}, u32[]{:S(2)}) %copy-start) | copy-done | bytes 2097176
  2.3 0.0 copy-start.2
  2.3 1.2 %copy-done.2 = bf16[1024,512]{1,0:T(8,128)(2,1)S(1)} copy-done((bf16[1024,512]{1,0:T(8,128)(2,1)S(1)}, bf16[1024,512]{1,0:T(8,128)(2,1)}, u32[]{:S(2)}) %copy-start.2) | copy-done | bytes 1048600
  3.5 0.0 copy-start.4
  3.5 0.8 %copy-done.4 = f32[2,8,1024]{2,1,0:T(8,128)S(1)} copy-done((f32[2,8,1024]{2,1,0:T(8,128)S(1)}, f32[2,8,1024]{2,1,0:T(8,128)}, u32[]{:S(2)}) %copy-start.4) | copy-done | bytes 65560
  4.4 53.5 %smoother.1 = (bf16[2,8,512,128]{3,2,1,0:T(8,128)(2,1)S(1)}, bf16[8,128,128]{2,1,0:T(8,128)(2,1)S(1)}) custom-call(bf16[2,8,512,128]{3,2,1,0:T(8,128)(2,1)S(1)} %copy-done, f32[2,8,1024]{2,1,0:T(8,128)S(1)} %copy-done.4, bf16[1024,512]{1,0:T(8,128)(2,1)S(1)} %copy-done.2, f32[2,1024]{1,0:T(2,128)S(1)} %multiply_multiply_fusion.wt_hbm), custom_call_target="tpu_custom_call" | custom-call | tf_op jit(solution)/shard_map/smoother/pallas_call | solution.py:376
  57.9 0.0 copy-start.1
  57.9 1.3 %copy-done.1 = bf16[2,8,512,128]{3,2,1,0:T(8,128)(2,1)} copy-done((bf16[2,8,512,128]{3,2,1,0:T(8,128)(2,1)}, bf16[2,8,512,128]{3,2,1,0:T(8,128)(2,1)S(1)}, u32[]{:S(2)}) %copy-start.1) | copy-done | bytes 2097176
  59.2 0.0 copy-start.3
  59.3 0.7 %copy-done.3 = bf16[8,128,128]{2,1,0:T(8,128)(2,1)} copy-done((bf16[8,128,128]{2,1,0:T(8,128)(2,1)}, bf16[8,128,128]{2,1,0:T(8,128)(2,1)S(1)}, u32[]{:S(2)}) %copy-start.3) | copy-done | bytes 262168
  60.0 7.0 %last_apply.1 = bf16[2,8,512,128]{3,2,1,0:T(8,128)(2,1)} custom-call(bf16[2,8,512,128]{3,2,1,0:T(8,128)(2,1)} %copy-done.1, bf16[8,128,128]{2,1,0:T(8,128)(2,1)} %copy-done.3), custom_call_target="tpu_custom_call" | custom-call | tf_op jit(solution)/shard_map/last_apply/pallas_call | solution.py:419
Async XLA Ops:
  0.7 1.6 %copy-start = (bf16[2,8,512,128]{3,2,1,0:T(8,128)(2,1)S(1)}, bf16[2,8,512,128]{3,2,1,0:T(8,128)(2,1)}, u32[]{:S(2)}) copy-start(bf16[2,8,512,128]{3,2,1,0:T(8,128)(2,1)} %x_hbm.1) | copy-start | bytes 6291460
  2.3 1.2 %copy-start.2 = (bf16[1024,512]{1,0:T(8,128)(2,1)S(1)}, bf16[1024,512]{1,0:T(8,128)(2,1)}, u32[]{:S(2)}) copy-start(bf16[1024,512]{1,0:T(8,128)(2,1)} %op_hbm.1) | copy-start | bytes 3145732
  3.5 0.8 %copy-start.4 = (f32[2,8,1024]{2,1,0:T(8,128)S(1)}, f32[2,8,1024]{2,1,0:T(8,128)}, u32[]{:S(2)}) copy-start(f32[2,8,1024]{2,1,0:T(8,128)} %obs_hbm.1) | copy-start | bytes 196612
  57.9 1.3 %copy-start.1 = (bf16[2,8,512,128]{3,2,1,0:T(8,128)(2,1)}, bf16[2,8,512,128]{3,2,1,0:T(8,128)(2,1)S(1)}, u32[]{:S(2)}) copy-start(bf16[2,8,512,128]{3,2,1,0:T(8,128)(2,1)S(1)} %get-tuple-element.7.x_ref) | copy-start | bytes 6291460
  59.2 0.7 %copy-start.3 = (bf16[8,128,128]{2,1,0:T(8,128)(2,1)}, bf16[8,128,128]{2,1,0:T(8,128)(2,1)S(1)}, u32[]{:S(2)}) copy-start(bf16[8,128,128]{2,1,0:T(8,128)(2,1)S(1)} %get-tuple-element.8.mix_ref) | copy-start | bytes 786436

commit v2 on v1

--- a/solution.py
+++ b/solution.py
@@ -111,12 +111,12 @@
 
 def kernel(
     regions,
-    x_hbm, obs_hbm, op_hbm, wt_hbm,
-    x1_hbm, mix_out,
-    xin, obs, op, wt, opw, amat, bvec,
-    sq, sc, dev, cen, zb, pk, x1t, x1v,
+    x_hbm, obs_hbm, op_hbm, prec_hbm, mask_hbm,
+    x1, mix_out,
+    xin, obs, op, prec, mask, wt, opw, amat, bvec,
+    sq, sc, dev, cen, zb, pk, x1t,
     halo_out, halo_in, part, rs_in, z_out, z_in, mixbuf,
-    load_sem, store_sem, halo_s, halo_r, rs_s, rs_r, z_s, z_r, ag_s, ag_r,
+    load_sem, halo_s, halo_r, rs_s, rs_r, z_s, z_r, ag_s, ag_r,
 ):
     slot, region = lax.axis_index("slot"), lax.axis_index("region")
     xi, zi = lax.rem(slot, XN), lax.div(slot, XN)
@@ -133,16 +133,20 @@
 
     loads = [
         pltpu.make_async_copy(op_hbm, op, load_sem.at[0]),
-        pltpu.make_async_copy(wt_hbm, wt, load_sem.at[1]),
-        pltpu.make_async_copy(obs_hbm, obs, load_sem.at[2]),
-        pltpu.make_async_copy(x_hbm.at[:, 0:1], xin.at[:, 0:1], load_sem.at[3]),
-        pltpu.make_async_copy(x_hbm.at[:, 7:8], xin.at[:, 1:2], load_sem.at[4]),
-        pltpu.make_async_copy(x_hbm.at[:, 1:7], xin.at[:, 2:8], load_sem.at[5]),
+        pltpu.make_async_copy(prec_hbm, prec, load_sem.at[1]),
+        pltpu.make_async_copy(mask_hbm, mask, load_sem.at[2]),
+        pltpu.make_async_copy(obs_hbm, obs, load_sem.at[3]),
+        pltpu.make_async_copy(x_hbm.at[:, 0:1], xin.at[:, 0:1], load_sem.at[4]),
+        pltpu.make_async_copy(x_hbm.at[:, 7:8], xin.at[:, 1:2], load_sem.at[5]),
+        pltpu.make_async_copy(x_hbm.at[:, 1:7], xin.at[:, 2:8], load_sem.at[6]),
     ]
     for load in loads:
         load.start()
-    for load in loads[:3]:
+    for load in loads[:4]:
         load.wait()
+    for ci in range(8):
+        cols = slice(ci * 128, (ci + 1) * 128)
+        wt[:, cols] = prec[ci:ci + 1, :] * mask[:, cols].astype(F32) * (1.0 / OUTER)
 
     @pl.loop(0, 8)
     def _(ci):
@@ -159,7 +163,7 @@
         for p in range(8):
             bvec[t, p] = both[p:p + 1] + both[p + 8:p + 9]
 
-    for load in loads[3:]:
+    for load in loads[4:]:
         load.wait()
 
     def squash(block, t, q, column):
@@ -239,10 +243,6 @@
             send_sem=ag_s.at[k, d - 1], recv_sem=ag_r.at[k, d - 1],
             device_id=(x_peer(d), region), device_id_type=MESH,
         )
-
-    def store(t, q):
-        p = 0 if q == 0 else 7 if q == 1 else q - 1
-        return pltpu.make_async_copy(x1v.at[t, q], x1_hbm.at[t, p], store_sem.at[t, q])
 
     for k in range(OUTER):
         @pl.loop(0, 4)
@@ -301,14 +301,12 @@
         if k == OUTER - 1:
             @pl.loop(0, 8)
             def _(q):
+                p = jnp.where(q == 0, 0, jnp.where(q == 1, 7, q - 1))
                 for t in range(2):
                     for column in range(4):
                         at = t * 512 + column * 128
                         block = x1t[q, :, at:at + 128].astype(F32).T
-                        x1v[t, q, column * 128:(column + 1) * 128, :] = block.astype(BF16)
-            for t in range(2):
-                for q in range(8):
-                    store(t, q).start()
+                        x1[t, p, column * 128:(column + 1) * 128, :] = block.astype(BF16)
 
         for d in range(1, XN):
             pltpu.make_async_remote_copy(
@@ -350,28 +348,29 @@
             ).wait_send()
             ag_copy(k, d).wait_send()
         z_copy(k).wait_send()
-    for t in range(2):
-        for q in range(8):
-            store(t, q).wait()
-
-
-def last_apply(x_ref, mix_ref, out_ref):
-    mix = mix_ref[0].astype(F32)
-    full = mix + (1.0 - jnp.sum(mix, axis=1, keepdims=True)) * (1.0 / 128)
-    high, low = halves(full)
-    for t in range(2):
-        x = x_ref[t, 0]
-        moved = lax.dot_general(x, low, NT, preferred_element_type=F32) + lax.dot_general(
-            x, high, NT, preferred_element_type=F32
-        )
-        out_ref[t, 0] = moved.astype(BF16)
+
+
+def last_apply(x_ref, mix_ref, out_hbm, out, sem):
+    def copy(p):
+        return pltpu.make_async_copy(out.at[:, p], out_hbm.at[:, p], sem.at[p])
+
+    for p in range(out.shape[1]):
+        mix = mix_ref[p].astype(F32)
+        full = mix + (1.0 - jnp.sum(mix, axis=1, keepdims=True)) * (1.0 / 128)
+        both = jnp.concatenate(halves(full), axis=1)
+        for t in range(2):
+            x = x_ref[t, p]
+            twice = jnp.concatenate([x, x], axis=1)
+            out[t, p] = lax.dot_general(twice, both, NT, preferred_element_type=F32).astype(BF16)
+        copy(p).start()
+    for p in range(out.shape[1]):
+        copy(p).wait()
 
 
 def shards(regions, ensemble, observations, operator_weight, obs_precision, channel_mask):
-    weights = obs_precision[None, :] * channel_mask.astype(F32) / OUTER
     slots, patches, rows, members = ensemble.shape
-    channels = operator_weight.shape[0]
-    anywhere = pl.BlockSpec(memory_space=pl.ANY)
+    hbm = pl.BlockSpec(memory_space=pltpu.HBM)
+    near = pl.BlockSpec(memory_space=pltpu.VMEM)
     dma, vmem = pltpu.SemaphoreType.DMA, pltpu.VMEM
     states, mixing = pl.pallas_call(
         functools.partial(kernel, regions),
@@ -379,12 +378,14 @@
             jax.ShapeDtypeStruct(ensemble.shape, BF16),
             jax.ShapeDtypeStruct((patches, members, members), BF16),
         ),
-        in_specs=[anywhere] * 4,
-        out_specs=(anywhere, pl.BlockSpec(memory_space=pltpu.VMEM)),
+        in_specs=[hbm] * 5,
+        out_specs=(near, near),
         scratch_shapes=[
             vmem((2, 8, 512, 128), BF16),
             vmem((2, 8, 1024), F32),
             vmem((1024, 512), BF16),
+            vmem((8, 128), F32),
+            vmem((2, 1024), jnp.int32),
             vmem((2, 1024), F32),
             vmem((2, 512, 1024), BF16),
             vmem((2, 512, 512), BF16),
@@ -396,7 +397,6 @@
             vmem((2, 144, 1024), BF16),
             vmem((8, 80, 128), F32),
             vmem((8, 128, 1024), BF16),
-            vmem((2, 8, 512, 128), BF16),
             vmem((2, 2, 80, 128), BF16),
             vmem((2, 2, 80, 128), BF16),
             vmem((2, XN, 2, 80, 128), BF16),
@@ -404,7 +404,7 @@
             vmem((2, 2, 80, 128), BF16),
             vmem((2, 2, 80, 128), BF16),
             vmem((2, 8, 128, 128), BF16),
-            dma((6,)), dma((2, 8)),
+            dma((7,)),
             dma((2, 2)), dma((2, 2)),
             dma((2, XN - 1)), dma((2, XN - 1)),
             dma((2,)), dma((2,)),
@@ -414,14 +414,21 @@
             collective_id=0, has_side_effects=True, vmem_limit_bytes=40 << 20
         ),
         name="smoother",
-    )(ensemble, observations, operator_weight, weights)
-    block = pl.BlockSpec((2, 1, rows, members), lambda p: (0, p, 0, 0))
+    )(
+        *(
+            pltpu.with_memory_space_constraint(array, pltpu.HBM)
+            for array in (
+                ensemble, observations, operator_weight, obs_precision.reshape(8, 128), channel_mask
+            )
+        )
+    )
     return pl.pallas_call(
         last_apply,
-        grid=(patches,),
         out_shape=jax.ShapeDtypeStruct(ensemble.shape, BF16),
-        in_specs=[block, pl.BlockSpec((1, members, members), lambda p: (p, 0, 0))],
-        out_specs=block,
+        in_specs=[near, near],
+        out_specs=hbm,
+        scratch_shapes=[vmem(ensemble.shape, BF16), dma((patches,))],
+        compiler_params=pltpu.CompilerParams(vmem_limit_bytes=16 << 20),
         name="last_apply",
     )(states, mixing)
 

time: 68.2 us -> 57 us (0.84)
  local copies, waits for them, and re-layouts: 5.69 us -> 0 us
  Pallas kernels: 60.5 us -> 56.2 us
  other arithmetic: 0.71 us -> 0 us
    unnamed x10 -> x0, local copies, waits for them, and re-layouts: 5.69 us -> none
    pallas_call x1, Pallas kernels: 7.01 us -> 2.13 us  [shards(): pl.pallas_call(last_apply, out_shape=jax.ShapeDtypeStruct(ensemble.shape,...]
    div x1 -> x0, other arithmetic: 0.71 us -> none  [shards(): weights = obs_precision[None, :] * channel_mask.astype(F32) / OUTER]
where the time goes in v2:
time: 57 us; the launch traced here: 56.2 us
  Pallas kernels  56.2 us (99%)
    pallas_call x1, Pallas kernels, shards(): pl.pallas_call(functools.partial(kernel, regions), out_shape=(jax.ShapeDt...  54.1 us
    pallas_call x1, Pallas kernels, shards(): pl.pallas_call(last_apply, out_shape=jax.ShapeDtypeStruct(ensemble.shape,...  2.13 us

profile of v2, /device:TPU:6, one launch (start us, length us, event | category | flops | bytes accessed | tf_op | source)
XLA Modules:
  0.0 56.2 jit_solution(1934663310947185828)
XLA Ops:
  0.0 54.1 %smoother.1 = (bf16[2,8,512,128]{3,2,1,0:T(8,128)(2,1)S(1)}, bf16[8,128,128]{2,1,0:T(8,128)(2,1)S(1)}) custom-call(bf16[2,8,512,128]{3,2,1,0:T(8,128)(2,1)} %x_hbm.1, f32[2,8,1024]{2,1,0:T(8,128)} %obs_hbm.1, bf16[1024,512]{1,0:T(8,128)(2,1)} %op_hbm.1, f32[8,128]{1,0:T(8,128)} %bitcast.1, s32[2,1024]{1,0:T(2,128)} %mask_hbm.1), custom_call_target="tpu_custom_call" | custom-call | tf_op jit(solution)/shard_map/smoother/pallas_call | solution.py:375
  54.1 2.1 %last_apply.1 = bf16[2,8,512,128]{3,2,1,0:T(8,128)(2,1)} custom-call(bf16[2,8,512,128]{3,2,1,0:T(8,128)(2,1)S(1)} %get-tuple-element.7.x_ref, bf16[8,128,128]{2,1,0:T(8,128)(2,1)S(1)} %get-tuple-element.8.mix_ref), custom_call_target="tpu_custom_call" | custom-call | tf_op jit(solution)/shard_map/last_apply/pallas_call | solution.py:425

commit v3 on v2

v3 whole, which is shorter than its diff:
```python
import functools
import math

import jax
import jax.numpy as jnp
from jax import lax
from jax.experimental import pallas as pl
from jax.experimental.pallas import tpu as pltpu
from jax.sharding import PartitionSpec as P

OUTER = 2
NS_STEPS = 8
LOCAL_WEIGHT = 0.5
XN = 4

F32 = jnp.float32
BF16 = jnp.bfloat16
MESH = pl.DeviceIdType.MESH
NT = (((1,), (1,)), ((), ()))


def iota(shape, dim):
    return lax.broadcasted_iota(jnp.int32, shape, dim)


def halves(a):
    high = a.astype(BF16)
    return high, (a - high.astype(F32)).astype(BF16)


def product(a, b):
    (ah, al), (bh, bl) = a, b
    return (
        jnp.dot(ah, bl, preferred_element_type=F32)
        + jnp.dot(al, bh, preferred_element_type=F32)
        + jnp.dot(ah, bh, preferred_element_type=F32)
    )


def packed(gram):
    top, bottom = gram[0:64], gram[64:128]
    row, col = iota((64, 128), 0), iota((64, 128), 1)
    body = jnp.where(col >= row, top, pltpu.roll(bottom, 64, 1))
    diag = jnp.sum(jnp.where(col == row + 64, bottom, 0.0), axis=0, keepdims=True)
    tail_row = iota((16, 128), 0)
    grad = gram[128:129] + gram[129:130]
    tail = jnp.where(tail_row == 0, diag, jnp.where(tail_row == 1, grad, 0.0))
    return jnp.concatenate([body, tail], axis=0)


def message(pack):
    tail = pack[64:80]
    row = iota((16, 128), 0)
    grad = tail[1:2] + tail[2:3]
    high = grad.astype(BF16).astype(F32)
    tail = jnp.where(
        row == 0, tail, jnp.where(row == 1, high, jnp.where(row == 2, grad - high, 0.0))
    )
    return jnp.concatenate([pack[0:64].astype(BF16), tail.astype(BF16)], axis=0)


def unpacked(pack):
    top = pack[0:64]
    row, col = iota((64, 128), 0), iota((64, 128), 1)
    upper = jnp.where(col >= row, top, 0.0)
    lower = pltpu.roll(jnp.where(col < row, top, 0.0), 64, 1)
    lower = jnp.where(col == row + 64, pack[64:65], lower)
    half = jnp.concatenate([upper, lower], axis=0)
    row, col = iota((128, 128), 0), iota((128, 128), 1)
    return jnp.where(row == col, half, half + half.T), pack[65:66] + pack[66:67]


def transforms(packs):
    members = 128
    row, col = iota((128, 128), 0), iota((128, 128), 1)
    identity = jnp.where(row == col, 1.0, 0.0).astype(F32)
    grads, scales, iterates, factors = [], [], [], []
    for pack in packs:
        gram, grad = unpacked(pack)
        shifted = gram + (members - 1.0) * identity
        total = jnp.sum(jnp.sum(shifted * shifted, axis=0, keepdims=True), axis=1, keepdims=True)
        norm = jnp.sqrt(total)
        grads.append(grad)
        scales.append(1.0 / jnp.sqrt(norm))
        iterates.append(shifted * (1.0 / norm))
    count = len(packs)
    middles = [1.5 * identity - 0.5 * it for it in iterates]
    split_mid = [halves(m) for m in middles]
    factors = middles
    iterates = [product(halves(iterates[i]), split_mid[i]) for i in range(count)]
    for number in range(1, NS_STEPS):
        split_fac = [halves(f) for f in factors]
        split_it = [halves(it) for it in iterates]
        middles = [
            1.5 * identity - 0.5 * product(split_fac[i], split_it[i]) for i in range(count)
        ]
        split_mid = [halves(m) for m in middles]
        if number + 1 < NS_STEPS:
            iterates = [product(split_it[i], split_mid[i]) for i in range(count)]
        factors = [product(split_mid[i], split_fac[i]) for i in range(count)]
    out = []
    for i in range(count):
        root = factors[i] * scales[i]
        split_root = halves(root)
        grad = jnp.broadcast_to(grads[i], (16, 128))
        inner = product(halves(grad), split_root)
        along = product(halves(inner), split_root)
        out.append((math.sqrt(members - 1.0) * root + along[0:1]).astype(BF16))
    return out


def pick(g, values):
    chosen = values[-1]
    for number in range(len(values) - 1):
        chosen = jnp.where(g == number, values[number], chosen)
    return chosen


def kernel(
    regions,
    x_hbm, obs_hbm, op_hbm, prec_hbm, mask_hbm,
    out,
    xin, obs, op, prec, mask, wt, opw, amat, bvec,
    xt, sq, sc, dev, cen, zb, pk, x1,
    halo_out, halo_in, part, rs_in, z_out, z_in, mixbuf,
    load_sem, halo_s, halo_r, rs_s, rs_r, z_s, z_r, ag_s, ag_r,
):
    slot, region = lax.axis_index("slot"), lax.axis_index("region")
    xi, zi = lax.rem(slot, XN), lax.div(slot, XN)
    z_peer = lax.rem(slot + XN, 2 * XN)
    before, after = lax.rem(region + regions - 1, regions), lax.rem(region + 1, regions)

    def at_x(j):
        return zi * XN + j

    def x_peer(d):
        return at_x(lax.rem(xi + d, XN))

    barrier = pltpu.get_barrier_semaphore()

    def greet(device):
        pl.semaphore_signal(barrier, inc=1, device_id=device, device_id_type=MESH)

    for d in range(1, XN):
        greet((x_peer(d), region))
    greet((z_peer, region))
    for edge, neighbour in ((0, before), (XN - 1, after)):
        @pl.when(xi == edge)
        def _():
            for j in range(XN):
                greet((at_x(j), neighbour))

    loads = [
        pltpu.make_async_copy(op_hbm, op, load_sem.at[0]),
        pltpu.make_async_copy(prec_hbm, prec, load_sem.at[1]),
        pltpu.make_async_copy(mask_hbm, mask, load_sem.at[2]),
        pltpu.make_async_copy(obs_hbm, obs, load_sem.at[3]),
        pltpu.make_async_copy(x_hbm, xin, load_sem.at[4]),
    ]
    for load in loads:
        load.start()
    pk[0] = jnp.zeros((80, 128), F32)
    pk[9] = jnp.zeros((80, 128), F32)
    for load in loads[:4]:
        load.wait()
    for ci in range(8):
        cols = slice(ci * 128, (ci + 1) * 128)
        wt[:, cols] = prec[ci:ci + 1, :] * mask[:, cols].astype(F32) * (1.0 / OUTER)

    @pl.loop(0, 8)
    def _(ci):
        c = pl.multiple_of(ci * 128, 128)
        weight = [wt[t:t + 1, pl.ds(c, 128)] for t in range(2)]
        for ri in range(4):
            block = op[pl.ds(c, 128), ri * 128:(ri + 1) * 128].astype(F32).T
            for t in range(2):
                opw[t, ri * 128:(ri + 1) * 128, pl.ds(c, 128)] = (block * weight[t]).astype(BF16)

    for t in range(2):
        high, low = halves(obs[t] * wt[t:t + 1, :])
        both = jnp.dot(jnp.concatenate([high, low], axis=0), op[...], preferred_element_type=F32)
        for p in range(8):
            bvec[t, p] = both[p:p + 1] + both[p + 8:p + 9]

    loads[4].wait()

    def squash(block, t, p, column):
        squashed = jnp.tanh(block).astype(BF16)
        wide = squashed.astype(F32)
        mean = jnp.sum(wide, axis=0, keepdims=True) * (1.0 / 128)
        sq[t, pl.ds(pl.multiple_of(p * 128, 128), 128), column * 128:(column + 1) * 128] = squashed
        at = t * 512 + column * 128
        sc[p, :, at:at + 128] = (wide - mean).astype(BF16)

    @pl.loop(0, 4)
    def _(step):
        t, first = lax.div(step, 2), pl.multiple_of(lax.rem(step, 2) * 256, 256)
        for i in range(2):
            cols = slice(i * 256, (i + 1) * 256)
            amat[t, pl.ds(first, 256), cols] = jnp.dot(
                opw[t, pl.ds(first, 256), :], op[:, cols], preferred_element_type=F32
            ).astype(BF16)
            p = 2 * step + i
            for s in range(2):
                for column in range(4):
                    block = xin[s, p, column * 128:(column + 1) * 128, :].astype(F32).T
                    xt[p, :, s * 512 + column * 128:s * 512 + (column + 1) * 128] = block.astype(BF16)
                    squash(block, s, p, column)

    def halo_copy(k, side):
        return pltpu.make_async_remote_copy(
            src_ref=halo_out.at[k, side], dst_ref=halo_in.at[k, xi],
            send_sem=halo_s.at[k, side], recv_sem=halo_r.at[k, xi],
            device_id=(at_x(XN - 1), before) if side == 0 else (at_x(0), after),
            device_id_type=MESH,
        )

    def halo_arrival(k, j):
        return pltpu.make_async_remote_copy(
            src_ref=halo_out.at[k, 0], dst_ref=halo_in.at[k, j],
            send_sem=halo_s.at[k, 0], recv_sem=halo_r.at[k, j],
            device_id=(at_x(0), after), device_id_type=MESH,
        )

    def rs_copy(k, d):
        return pltpu.make_async_remote_copy(
            src_ref=part.at[k, d - 1], dst_ref=rs_in.at[k, d - 1],
            send_sem=rs_s.at[k, d - 1], recv_sem=rs_r.at[k, d - 1],
            device_id=(x_peer(d), region), device_id_type=MESH,
        )

    def localized(p):
        return pk[p + 1] + LOCAL_WEIGHT * (pk[p] + pk[p + 2])

    def send_share(k, d):
        j = lax.rem(xi + d, XN)
        for i in range(2):
            part[k, d - 1, i] = message(localized(2 * j + i))
        rs_copy(k, d).start()

    def z_copy(k):
        return pltpu.make_async_remote_copy(
            src_ref=z_out.at[k], dst_ref=z_in.at[k], send_sem=z_s.at[k], recv_sem=z_r.at[k],
            device_id=(z_peer, region), device_id_type=MESH,
        )

    def ag_copy(k, d):
        own = pl.ds(2 * xi, 2)
        return pltpu.make_async_remote_copy(
            src_ref=mixbuf.at[k, own], dst_ref=mixbuf.at[k, own],
            send_sem=ag_s.at[k, d - 1], recv_sem=ag_r.at[k, d - 1],
            device_id=(x_peer(d), region), device_id_type=MESH,
        )

    def await_pair(k, g):
        ahead = pick(g, (0, 1, 3, 2))

        @pl.when(g > 0)
        def _():
            d = XN - ahead
            other = pl.ds(2 * lax.rem(xi + ahead, XN), 2)
            pltpu.make_async_remote_copy(
                src_ref=mixbuf.at[k, other], dst_ref=mixbuf.at[k, other],
                send_sem=ag_s.at[k, d - 1], recv_sem=ag_r.at[k, d - 1],
                device_id=(x_peer(1), region), device_id_type=MESH,
            ).wait_recv()

        return lax.rem(xi + ahead, XN)

    for k in range(OUTER):
        @pl.loop(0, 4)
        def _(g):
            if k > 0:
                j = await_pair(k - 1, g)
                for i in range(2):
                    p = 2 * j + i
                    moved = jnp.dot(mixbuf[k - 1, p], dev[p], preferred_element_type=F32)
                    for t in range(2):
                        for column in range(4):
                            at = t * 512 + column * 128
                            rounded = (cen[p, :, at:at + 128] + moved[:, at:at + 128]).astype(BF16)
                            xt[p, :, at:at + 128] = rounded
                            squash(rounded.astype(F32), t, p, column)
            else:
                j = pick(g, (0, 3, 1, 2))
            for t in range(2):
                lines = pl.ds(pl.multiple_of(j * 256, 256), 256)
                for n in range(2):
                    cols = slice(n * 256, (n + 1) * 256)
                    applied = jnp.dot(sq[t, lines, :], amat[t, :, cols], preferred_element_type=F32)
                    for i in range(2):
                        z = applied[i * 128:(i + 1) * 128]
                        mean = jnp.sum(z, axis=0, keepdims=True) * (1.0 / 128)
                        at = t * 512 + n * 256
                        zb[i, 0:128, at:at + 256] = (z - mean).astype(BF16)
                        pull = bvec[t, 2 * j + i, :, cols] - mean
                        high = pull.astype(BF16).astype(F32)
                        row = iota((16, 256), 0)
                        tail = jnp.where(row == 0, high, jnp.where(row == 1, pull - high, 0.0))
                        zb[i, 128:144, at:at + 256] = tail.astype(BF16)
            for i in range(2):
                p = 2 * j + i
                gram = lax.dot_general(zb[i], sc[p], NT, preferred_element_type=F32)
                pk[p + 1] = packed(gram)

            if k == 0:
                @pl.when(g == 0)
                def _():
                    pl.semaphore_wait(barrier, XN + 2)

            for side, edge in ((0, 0), (1, XN - 1)):
                @pl.when(j == edge)
                def _():
                    halo_out[k, side] = message(pk[1 + 7 * side])
                    halo_copy(k, side).start()

        for d in (2, 1, 3):
            send_share(k, d)

        if k == 0:
            @pl.loop(0, 8)
            def _(p):
                for column in range(8):
                    cols = slice(column * 128, (column + 1) * 128)
                    block = xt[p, :, cols].astype(F32)
                    centre = jnp.sum(block, axis=0, keepdims=True) * (1.0 / 128)
                    cen[p, :, cols] = centre
                    dev[p, :, cols] = (block - centre).astype(BF16)
        else:
            @pl.loop(0, 8)
            def _(p):
                for t in range(2):
                    for column in range(4):
                        at = t * 512 + column * 128
                        block = xt[p, :, at:at + 128].astype(F32).T
                        x1[t, p, column * 128:(column + 1) * 128, :] = block.astype(BF16)

        sums = [localized(2 * xi + i) for i in range(2)]
        for d in (1, 3, 2):
            rs_copy(k, d).wait_recv()
            for i in range(2):
                sums[i] = sums[i] + rs_in[k, d - 1, i].astype(F32)
        for i in range(2):
            pk[10 + i] = sums[i]
        for edge, i in ((0, 0), (XN - 1, 1)):
            @pl.when(xi == edge)
            def _():
                total = pk[10 + i]
                for j in range(XN):
                    halo_arrival(k, j).wait_recv()
                    total = total + LOCAL_WEIGHT * halo_in[k, j].astype(F32)
                pk[10 + i] = total
        for i in range(2):
            z_out[k, i] = message(pk[10 + i])
        z_copy(k).start()
        z_copy(k).wait_recv()
        mixes = transforms([pk[10 + i] + z_in[k, i].astype(F32) for i in range(2)])
        for i in range(2):
            mixbuf[k, 2 * xi + i] = mixes[i]
        for d in (2, 1, 3):
            ag_copy(k, d).start()

    @pl.loop(0, 4)
    def _(g):
        j = await_pair(OUTER - 1, g)
        for i in range(2):
            p = 2 * j + i
            mix = mixbuf[OUTER - 1, p].astype(F32)
            full = mix + (1.0 - jnp.sum(mix, axis=1, keepdims=True)) * (1.0 / 128)
            both = jnp.concatenate(halves(full), axis=1)
            for t in range(2):
                x = x1[t, p]
                twice = jnp.concatenate([x, x], axis=1)
                moved = lax.dot_general(twice, both, NT, preferred_element_type=F32)
                out[t, p] = moved.astype(BF16)

    for k in range(OUTER):
        for side in range(2):
            halo_copy(k, side).wait_send()
        for d in range(1, XN):
            rs_copy(k, d).wait_send()
            ag_copy(k, d).wait_send()
        z_copy(k).wait_send()


def shards(regions, ensemble, observations, operator_weight, obs_precision, channel_mask):
    slots, patches, rows, members = ensemble.shape
    hbm = pl.BlockSpec(memory_space=pltpu.HBM)
    near = pl.BlockSpec(memory_space=pltpu.VMEM)
    dma, vmem = pltpu.SemaphoreType.DMA, pltpu.VMEM
    return pl.pallas_call(
        functools.partial(kernel, regions),
        out_shape=jax.ShapeDtypeStruct(ensemble.shape, BF16),
        in_specs=[hbm] * 5,
        out_specs=near,
        scratch_shapes=[
            vmem((2, 8, 512, 128), BF16),
            vmem((2, 8, 1024), F32),
            vmem((1024, 512), BF16),
            vmem((8, 128), F32),
            vmem((2, 1024), jnp.int32),
            vmem((2, 1024), F32),
            vmem((2, 512, 1024), BF16),
            vmem((2, 512, 512), BF16),
            vmem((2, 8, 1, 512), F32),
            vmem((8, 128, 1024), BF16),
            vmem((2, 1024, 512), BF16),
            vmem((8, 128, 1024), BF16),
            vmem((8, 128, 1024), BF16),
            vmem((8, 1, 1024), F32),
            vmem((2, 144, 1024), BF16),
            vmem((12, 80, 128), F32),
            vmem((2, 8, 512, 128), BF16),
            vmem((2, 2, 80, 128), BF16),
            vmem((2, XN, 80, 128), BF16),
            vmem((2, XN - 1, 2, 80, 128), BF16),
            vmem((2, XN - 1, 2, 80, 128), BF16),
            vmem((2, 2, 80, 128), BF16),
            vmem((2, 2, 80, 128), BF16),
            vmem((2, 8, 128, 128), BF16),
            dma((5,)),
            dma((2, 2)), dma((2, XN)),
            dma((2, XN - 1)), dma((2, XN - 1)),
            dma((2,)), dma((2,)),
            dma((2, XN - 1)), dma((2, XN - 1)),
        ],
        compiler_params=pltpu.CompilerParams(
            collective_id=0, has_side_effects=True, vmem_limit_bytes=40 << 20
        ),
        name="smoother",
    )(
        *(
            pltpu.with_memory_space_constraint(array, pltpu.HBM)
            for array in (
                ensemble, observations, operator_weight, obs_precision.reshape(8, 128), channel_mask
            )
        )
    )


def solution(mesh):
    return jax.shard_map(
        functools.partial(shards, mesh.shape["region"]),
        mesh=mesh,
        in_specs=(
            P("slot", "region", None, None),
            P("slot", "region", None),
            P(),
            P(),
            P("slot", None),
        ),
        out_specs=P("slot", "region", None, None),
        check_vma=False,
    )
```

time: 57 us -> 53.2 us (0.933); the launches traced: 56.2 us -> 53.1 us
  Pallas kernels: 56.2 us -> 51.8 us
  local copies, waits for them, and re-layouts: 0 us -> 1.32 us
    pallas_call x2 -> x1, Pallas kernels: 56.2 us -> 51.8 us  [shards(): pl.pallas_call(functools.partial(kernel, regions), out_shape=jax.ShapeDty...]
    unnamed x0 -> x1, local copies, waits for them, and re-layouts: none -> 1.32 us
where the time goes in v3:
time: 53.2 us; the launch traced here: 53.1 us
  Pallas kernels  51.8 us (97%)
  local copies, waits for them, and re-layouts  1.32 us (2%)
    pallas_call x1, Pallas kernels, shards(): pl.pallas_call(functools.partial(kernel, regions), out_shape=jax.ShapeDty...  51.8 us
    unnamed x1, local copies, waits for them, and re-layouts  1.32 us

profile of v3, /device:TPU:6, one launch (start us, length us, event | category | flops | bytes accessed | tf_op | source)
XLA Modules:
  0.0 53.1 jit_solution(176232113015624988)
XLA Ops:
  0.0 51.8 %smoother.1 = bf16[2,8,512,128]{3,2,1,0:T(8,128)(2,1)S(1)} custom-call(bf16[2,8,512,128]{3,2,1,0:T(8,128)(2,1)} %x_hbm.1, f32[2,8,1024]{2,1,0:T(8,128)} %obs_hbm.1, bf16[1024,512]{1,0:T(8,128)(2,1)} %op_hbm.1, f32[8,128]{1,0:T(8,128)} %bitcast.1, s32[2,1024]{1,0:T(2,128)} %mask_hbm.1), custom_call_target="tpu_custom_call" | custom-call | tf_op jit(solution)/shard_map/smoother/pallas_call | solution.py:391
  51.8 1.3 %copy.7 = bf16[2,8,512,128]{3,2,1,0:T(8,128)(2,1)} copy(bf16[2,8,512,128]{3,2,1,0:T(8,128)(2,1)S(1)} %smoother.1) | data formatting | bytes 4194304

commit v4 on v3

--- a/solution.py
+++ b/solution.py
@@ -30,20 +30,30 @@
 
 def product(a, b):
     (ah, al), (bh, bl) = a, b
-    return (
-        jnp.dot(ah, bl, preferred_element_type=F32)
-        + jnp.dot(al, bh, preferred_element_type=F32)
-        + jnp.dot(ah, bh, preferred_element_type=F32)
+    left = jnp.concatenate([ah, al], axis=1)
+    right = jnp.concatenate(
+        [jnp.concatenate([bh, bl], axis=1), jnp.concatenate([bh, jnp.zeros_like(bl)], axis=1)],
+        axis=0,
     )
-
-
-def packed(gram):
+    both = jnp.dot(left, right, preferred_element_type=F32)
+    return both[:, 0:128] + both[:, 128:256]
+
+
+def first_term(a, b):
+    return jnp.dot(a[0], b[0], preferred_element_type=F32)
+
+
+def packed(raw):
+    first = jnp.sum(raw[0:128], axis=0, keepdims=True) * (1.0 / 128)
+    pull = jnp.broadcast_to(raw[128:129] + raw[129:130], (8, 128))
+    gram = jnp.concatenate([raw[0:128], pull], axis=0) - first
+    gram = gram - jnp.sum(gram, axis=1, keepdims=True) * (1.0 / 128)
     top, bottom = gram[0:64], gram[64:128]
     row, col = iota((64, 128), 0), iota((64, 128), 1)
     body = jnp.where(col >= row, top, pltpu.roll(bottom, 64, 1))
     diag = jnp.sum(jnp.where(col == row + 64, bottom, 0.0), axis=0, keepdims=True)
     tail_row = iota((16, 128), 0)
-    grad = gram[128:129] + gram[129:130]
+    grad = gram[128:129]
     tail = jnp.where(tail_row == 0, diag, jnp.where(tail_row == 1, grad, 0.0))
     return jnp.concatenate([body, tail], axis=0)
 
@@ -91,8 +101,9 @@
     for number in range(1, NS_STEPS):
         split_fac = [halves(f) for f in factors]
         split_it = [halves(it) for it in iterates]
+        multiply = first_term if number < NS_STEPS - 2 else product
         middles = [
-            1.5 * identity - 0.5 * product(split_fac[i], split_it[i]) for i in range(count)
+            1.5 * identity - 0.5 * multiply(split_fac[i], split_it[i]) for i in range(count)
         ]
         split_mid = [halves(m) for m in middles]
         if number + 1 < NS_STEPS:
@@ -120,8 +131,8 @@
     regions,
     x_hbm, obs_hbm, op_hbm, prec_hbm, mask_hbm,
     out,
-    xin, obs, op, prec, mask, wt, opw, amat, bvec,
-    xt, sq, sc, dev, cen, zb, pk, x1,
+    xin, obs, op, prec, mask, wt, opw, amat,
+    sr, sq, dev, cen, zb, pk, x1,
     halo_out, halo_in, part, rs_in, z_out, z_in, mixbuf,
     load_sem, halo_s, halo_r, rs_s, rs_r, z_s, z_r, ag_s, ag_r,
 ):
@@ -179,18 +190,14 @@
     for t in range(2):
         high, low = halves(obs[t] * wt[t:t + 1, :])
         both = jnp.dot(jnp.concatenate([high, low], axis=0), op[...], preferred_element_type=F32)
+        row = iota((16, 512), 0)
         for p in range(8):
-            bvec[t, p] = both[p:p + 1] + both[p + 8:p + 9]
+            pull = both[p:p + 1] + both[p + 8:p + 9]
+            high = pull.astype(BF16).astype(F32)
+            tail = jnp.where(row == 0, high, jnp.where(row == 1, pull - high, 0.0))
+            zb[p, 128:144, t * 512:(t + 1) * 512] = tail.astype(BF16)
 
     loads[4].wait()
-
-    def squash(block, t, p, column):
-        squashed = jnp.tanh(block).astype(BF16)
-        wide = squashed.astype(F32)
-        mean = jnp.sum(wide, axis=0, keepdims=True) * (1.0 / 128)
-        sq[t, pl.ds(pl.multiple_of(p * 128, 128), 128), column * 128:(column + 1) * 128] = squashed
-        at = t * 512 + column * 128
-        sc[p, :, at:at + 128] = (wide - mean).astype(BF16)
 
     @pl.loop(0, 4)
     def _(step):
@@ -203,9 +210,10 @@
             p = 2 * step + i
             for s in range(2):
                 for column in range(4):
-                    block = xin[s, p, column * 128:(column + 1) * 128, :].astype(F32).T
-                    xt[p, :, s * 512 + column * 128:s * 512 + (column + 1) * 128] = block.astype(BF16)
-                    squash(block, s, p, column)
+                    rows = slice(column * 128, (column + 1) * 128)
+                    squashed = jnp.tanh(xin[s, p, rows, :].astype(F32))
+                    sr[s, p, rows, :] = squashed.astype(BF16)
+                    sq[s, pl.ds(pl.multiple_of(p * 128, 128), 128), rows] = squashed.T.astype(BF16)
 
     def halo_copy(k, side):
         return pltpu.make_async_remote_copy(
@@ -267,10 +275,30 @@
 
         return lax.rem(xi + ahead, XN)
 
+    def weigh(j):
+        for t in range(2):
+            lines = pl.ds(pl.multiple_of(j * 256, 256), 256)
+            for n in range(2):
+                cols = slice(n * 256, (n + 1) * 256)
+                applied = jnp.dot(sq[t, lines, :], amat[t, :, cols], preferred_element_type=F32)
+                for i in range(2):
+                    at = t * 512 + n * 256
+                    z = applied[i * 128:(i + 1) * 128]
+                    zb[2 * j + i, 0:128, at:at + 256] = z.astype(BF16)
+
+    def quad(p):
+        raw = jnp.dot(zb[p, :, 0:512], sr[0, p], preferred_element_type=F32) + jnp.dot(
+            zb[p, :, 512:1024], sr[1, p], preferred_element_type=F32
+        )
+        pk[p + 1] = packed(raw)
+
     for k in range(OUTER):
-        @pl.loop(0, 4)
-        def _(g):
-            if k > 0:
+        if k == 0:
+            for j in range(4):
+                weigh(j)
+        else:
+            @pl.loop(0, 4)
+            def _(g):
                 j = await_pair(k - 1, g)
                 for i in range(2):
                     p = 2 * j + i
@@ -278,62 +306,41 @@
                     for t in range(2):
                         for column in range(4):
                             at = t * 512 + column * 128
+                            rows = slice(column * 128, (column + 1) * 128)
                             rounded = (cen[p, :, at:at + 128] + moved[:, at:at + 128]).astype(BF16)
-                            xt[p, :, at:at + 128] = rounded
-                            squash(rounded.astype(F32), t, p, column)
-            else:
-                j = pick(g, (0, 3, 1, 2))
-            for t in range(2):
-                lines = pl.ds(pl.multiple_of(j * 256, 256), 256)
-                for n in range(2):
-                    cols = slice(n * 256, (n + 1) * 256)
-                    applied = jnp.dot(sq[t, lines, :], amat[t, :, cols], preferred_element_type=F32)
-                    for i in range(2):
-                        z = applied[i * 128:(i + 1) * 128]
-                        mean = jnp.sum(z, axis=0, keepdims=True) * (1.0 / 128)
-                        at = t * 512 + n * 256
-                        zb[i, 0:128, at:at + 256] = (z - mean).astype(BF16)
-                        pull = bvec[t, 2 * j + i, :, cols] - mean
-                        high = pull.astype(BF16).astype(F32)
-                        row = iota((16, 256), 0)
-                        tail = jnp.where(row == 0, high, jnp.where(row == 1, pull - high, 0.0))
-                        zb[i, 128:144, at:at + 256] = tail.astype(BF16)
-            for i in range(2):
-                p = 2 * j + i
-                gram = lax.dot_general(zb[i], sc[p], NT, preferred_element_type=F32)
-                pk[p + 1] = packed(gram)
-
-            if k == 0:
-                @pl.when(g == 0)
-                def _():
-                    pl.semaphore_wait(barrier, XN + 2)
-
-            for side, edge in ((0, 0), (1, XN - 1)):
-                @pl.when(j == edge)
-                def _():
-                    halo_out[k, side] = message(pk[1 + 7 * side])
-                    halo_copy(k, side).start()
+                            block = rounded.astype(F32)
+                            sq[t, pl.ds(pl.multiple_of(p * 128, 128), 128), rows] = jnp.tanh(
+                                block
+                            ).astype(BF16)
+                            block = block.T
+                            x1[t, p, rows, :] = block.astype(BF16)
+                            sr[t, p, rows, :] = jnp.tanh(block).astype(BF16)
+                weigh(j)
+
+        for p in (0, 7):
+            quad(p)
+        for side in range(2):
+            halo_out[k, side] = message(pk[1 + 7 * side])
+        if k == 0:
+            pl.semaphore_wait(barrier, XN + 2)
+        for side in range(2):
+            halo_copy(k, side).start()
+        for p in range(1, 7):
+            quad(p)
 
         for d in (2, 1, 3):
             send_share(k, d)
 
         if k == 0:
-            @pl.loop(0, 8)
-            def _(p):
-                for column in range(8):
-                    cols = slice(column * 128, (column + 1) * 128)
-                    block = xt[p, :, cols].astype(F32)
-                    centre = jnp.sum(block, axis=0, keepdims=True) * (1.0 / 128)
-                    cen[p, :, cols] = centre
-                    dev[p, :, cols] = (block - centre).astype(BF16)
-        else:
             @pl.loop(0, 8)
             def _(p):
                 for t in range(2):
                     for column in range(4):
+                        block = xin[t, p, column * 128:(column + 1) * 128, :].astype(F32).T
+                        centre = jnp.sum(block, axis=0, keepdims=True) * (1.0 / 128)
                         at = t * 512 + column * 128
-                        block = xt[p, :, at:at + 128].astype(F32).T
-                        x1[t, p, column * 128:(column + 1) * 128, :] = block.astype(BF16)
+                        cen[p, :, at:at + 128] = centre
+                        dev[p, :, at:at + 128] = (block - centre).astype(BF16)
 
         sums = [localized(2 * xi + i) for i in range(2)]
         for d in (1, 3, 2):
@@ -402,13 +409,11 @@
             vmem((2, 1024), F32),
             vmem((2, 512, 1024), BF16),
             vmem((2, 512, 512), BF16),
-            vmem((2, 8, 1, 512), F32),
-            vmem((8, 128, 1024), BF16),
+            vmem((2, 8, 512, 128), BF16),
             vmem((2, 1024, 512), BF16),
             vmem((8, 128, 1024), BF16),
-            vmem((8, 128, 1024), BF16),
             vmem((8, 1, 1024), F32),
-            vmem((2, 144, 1024), BF16),
+            vmem((8, 144, 1024), BF16),
             vmem((12, 80, 128), F32),
             vmem((2, 8, 512, 128), BF16),
             vmem((2, 2, 80, 128), BF16),

time: 53.2 us -> 51.8 us (0.974)
  Pallas kernels: 51.8 us -> 50.4 us
    pallas_call x1, Pallas kernels: 51.8 us -> 50.4 us  [shards(): pl.pallas_call(functools.partial(kernel, regions), out_shape=jax.ShapeDty...]
where the time goes in v4:
time: 51.8 us; the launch traced here: 51.7 us
  Pallas kernels  50.4 us (97%)
  local copies, waits for them, and re-layouts  1.32 us (3%)
    pallas_call x1, Pallas kernels, shards(): pl.pallas_call(functools.partial(kernel, regions), out_shape=jax.ShapeDty...  50.4 us
    unnamed x1, local copies, waits for them, and re-layouts  1.32 us

profile of v4, /device:TPU:6, one launch (start us, length us, event | category | flops | bytes accessed | tf_op | source)
XLA Modules:
  0.0 51.7 jit_solution(11681536669222191810)
XLA Ops:
  0.0 50.4 %smoother.1 = bf16[2,8,512,128]{3,2,1,0:T(8,128)(2,1)S(1)} custom-call(bf16[2,8,512,128]{3,2,1,0:T(8,128)(2,1)} %x_hbm.1, f32[2,8,1024]{2,1,0:T(8,128)} %obs_hbm.1, bf16[1024,512]{1,0:T(8,128)(2,1)} %op_hbm.1, f32[8,128]{1,0:T(8,128)} %bitcast.1, s32[2,1024]{1,0:T(2,128)} %mask_hbm.1), custom_call_target="tpu_custom_call" | custom-call | tf_op jit(solution)/shard_map/smoother/pallas_call | solution.py:398
  50.4 1.3 %copy.7 = bf16[2,8,512,128]{3,2,1,0:T(8,128)(2,1)} copy(bf16[2,8,512,128]{3,2,1,0:T(8,128)(2,1)S(1)} %smoother.1) | data formatting | bytes 4194304

commit v5 on v4

--- a/solution.py
+++ b/solution.py
@@ -97,26 +97,31 @@
     middles = [1.5 * identity - 0.5 * it for it in iterates]
     split_mid = [halves(m) for m in middles]
     factors = middles
-    iterates = [product(halves(iterates[i]), split_mid[i]) for i in range(count)]
+    iterates = [
+        product(
+            halves(jnp.concatenate([iterates[i], jnp.broadcast_to(grads[i], (16, 128))], axis=0)),
+            split_mid[i],
+        )
+        for i in range(count)
+    ]
     for number in range(1, NS_STEPS):
         split_fac = [halves(f) for f in factors]
         split_it = [halves(it) for it in iterates]
         multiply = first_term if number < NS_STEPS - 2 else product
         middles = [
-            1.5 * identity - 0.5 * multiply(split_fac[i], split_it[i]) for i in range(count)
+            1.5 * identity
+            - 0.5 * multiply(split_fac[i], tuple(part[0:128] for part in split_it[i]))
+            for i in range(count)
         ]
         split_mid = [halves(m) for m in middles]
-        if number + 1 < NS_STEPS:
-            iterates = [product(split_it[i], split_mid[i]) for i in range(count)]
+        if number + 1 == NS_STEPS:
+            split_it = [tuple(part[128:144] for part in split) for split in split_it]
+        iterates = [product(split_it[i], split_mid[i]) for i in range(count)]
         factors = [product(split_mid[i], split_fac[i]) for i in range(count)]
     out = []
     for i in range(count):
-        root = factors[i] * scales[i]
-        split_root = halves(root)
-        grad = jnp.broadcast_to(grads[i], (16, 128))
-        inner = product(halves(grad), split_root)
-        along = product(halves(inner), split_root)
-        out.append((math.sqrt(members - 1.0) * root + along[0:1]).astype(BF16))
+        along = product(halves(iterates[i]), halves(factors[i]))[0:1] * (scales[i] * scales[i])
+        out.append((math.sqrt(members - 1.0) * scales[i] * factors[i] + along).astype(BF16))
     return out
 
 
@@ -134,7 +139,7 @@
     xin, obs, op, prec, mask, wt, opw, amat,
     sr, sq, dev, cen, zb, pk, x1,
     halo_out, halo_in, part, rs_in, z_out, z_in, mixbuf,
-    load_sem, halo_s, halo_r, rs_s, rs_r, z_s, z_r, ag_s, ag_r,
+    load_sem, op_sem, halo_s, halo_r, rs_s, rs_r, z_s, z_r, ag_s, ag_r,
 ):
     slot, region = lax.axis_index("slot"), lax.axis_index("region")
     xi, zi = lax.rem(slot, XN), lax.div(slot, XN)
@@ -161,18 +166,25 @@
             for j in range(XN):
                 greet((at_x(j), neighbour))
 
+    def op_load(ci):
+        lines = pl.ds(pl.multiple_of(ci * 128, 128), 128)
+        return pltpu.make_async_copy(op_hbm.at[lines], op.at[lines], op_sem.at[ci])
+
     loads = [
-        pltpu.make_async_copy(op_hbm, op, load_sem.at[0]),
-        pltpu.make_async_copy(prec_hbm, prec, load_sem.at[1]),
-        pltpu.make_async_copy(mask_hbm, mask, load_sem.at[2]),
-        pltpu.make_async_copy(obs_hbm, obs, load_sem.at[3]),
-        pltpu.make_async_copy(x_hbm, xin, load_sem.at[4]),
+        pltpu.make_async_copy(prec_hbm, prec, load_sem.at[0]),
+        pltpu.make_async_copy(mask_hbm, mask, load_sem.at[1]),
+        pltpu.make_async_copy(obs_hbm, obs, load_sem.at[2]),
+        pltpu.make_async_copy(x_hbm, xin, load_sem.at[3]),
     ]
-    for load in loads:
+    for load in loads[:2]:
+        load.start()
+    for ci in range(8):
+        op_load(ci).start()
+    for load in loads[2:]:
         load.start()
     pk[0] = jnp.zeros((80, 128), F32)
     pk[9] = jnp.zeros((80, 128), F32)
-    for load in loads[:4]:
+    for load in loads[:2]:
         load.wait()
     for ci in range(8):
         cols = slice(ci * 128, (ci + 1) * 128)
@@ -180,6 +192,7 @@
 
     @pl.loop(0, 8)
     def _(ci):
+        op_load(ci).wait()
         c = pl.multiple_of(ci * 128, 128)
         weight = [wt[t:t + 1, pl.ds(c, 128)] for t in range(2)]
         for ri in range(4):
@@ -187,6 +200,7 @@
             for t in range(2):
                 opw[t, ri * 128:(ri + 1) * 128, pl.ds(c, 128)] = (block * weight[t]).astype(BF16)
 
+    loads[2].wait()
     for t in range(2):
         high, low = halves(obs[t] * wt[t:t + 1, :])
         both = jnp.dot(jnp.concatenate([high, low], axis=0), op[...], preferred_element_type=F32)
@@ -197,7 +211,7 @@
             tail = jnp.where(row == 0, high, jnp.where(row == 1, pull - high, 0.0))
             zb[p, 128:144, t * 512:(t + 1) * 512] = tail.astype(BF16)
 
-    loads[4].wait()
+    loads[3].wait()
 
     @pl.loop(0, 4)
     def _(step):
@@ -292,10 +306,20 @@
         )
         pk[p + 1] = packed(raw)
 
+    def send_edge(k, side):
+        quad(7 * side)
+        halo_out[k, side] = message(pk[1 + 7 * side])
+        halo_copy(k, side).start()
+
     for k in range(OUTER):
         if k == 0:
-            for j in range(4):
-                weigh(j)
+            weigh(0)
+            weigh(3)
+            pl.semaphore_wait(barrier, XN + 2)
+            for side in range(2):
+                send_edge(k, side)
+            weigh(1)
+            weigh(2)
         else:
             @pl.loop(0, 4)
             def _(g):
@@ -316,15 +340,11 @@
                             x1[t, p, rows, :] = block.astype(BF16)
                             sr[t, p, rows, :] = jnp.tanh(block).astype(BF16)
                 weigh(j)
-
-        for p in (0, 7):
-            quad(p)
-        for side in range(2):
-            halo_out[k, side] = message(pk[1 + 7 * side])
-        if k == 0:
-            pl.semaphore_wait(barrier, XN + 2)
-        for side in range(2):
-            halo_copy(k, side).start()
+                for side in range(2):
+                    @pl.when(j == side * (XN - 1))
+                    def _():
+                        send_edge(k, side)
+
         for p in range(1, 7):
             quad(p)
 
@@ -423,7 +443,7 @@
             vmem((2, 2, 80, 128), BF16),
             vmem((2, 2, 80, 128), BF16),
             vmem((2, 8, 128, 128), BF16),
-            dma((5,)),
+            dma((4,)), dma((8,)),
             dma((2, 2)), dma((2, XN)),
             dma((2, XN - 1)), dma((2, XN - 1)),
             dma((2,)), dma((2,)),

time: 51.8 us -> 50.7 us (0.979)
  Pallas kernels: 50.4 us -> 49.3 us
    pallas_call x1, Pallas kernels: 50.4 us -> 49.3 us  [shards(): pl.pallas_call(functools.partial(kernel, regions), out_shape=jax.ShapeDty...]
where the time goes in v5:
time: 50.7 us
  Pallas kernels  49.3 us (97%)
  local copies, waits for them, and re-layouts  1.32 us (3%)
    pallas_call x1, Pallas kernels, shards(): pl.pallas_call(functools.partial(kernel, regions), out_shape=jax.ShapeDty...  49.3 us
    unnamed x1, local copies, waits for them, and re-layouts  1.32 us

profile of v5, /device:TPU:6, one launch (start us, length us, event | category | flops | bytes accessed | tf_op | source)
XLA Modules:
  0.0 50.7 jit_solution(7984190113745187307)
XLA Ops:
  0.0 49.3 %smoother.1 = bf16[2,8,512,128]{3,2,1,0:T(8,128)(2,1)S(1)} custom-call(bf16[2,8,512,128]{3,2,1,0:T(8,128)(2,1)} %x_hbm.1, f32[2,8,1024]{2,1,0:T(8,128)} %obs_hbm.1, bf16[1024,512]{1,0:T(8,128)(2,1)} %op_hbm.1, f32[8,128]{1,0:T(8,128)} %bitcast.1, s32[2,1024]{1,0:T(2,128)} %mask_hbm.1), custom_call_target="tpu_custom_call" | custom-call | tf_op jit(solution)/shard_map/smoother/pallas_call | solution.py:418
  49.3 1.3 %copy.7 = bf16[2,8,512,128]{3,2,1,0:T(8,128)(2,1)} copy(bf16[2,8,512,128]{3,2,1,0:T(8,128)(2,1)S(1)} %smoother.1) | data formatting | bytes 4194304

commit v6 on v5

--- a/solution.py
+++ b/solution.py
@@ -340,10 +340,9 @@
                             x1[t, p, rows, :] = block.astype(BF16)
                             sr[t, p, rows, :] = jnp.tanh(block).astype(BF16)
                 weigh(j)
-                for side in range(2):
-                    @pl.when(j == side * (XN - 1))
-                    def _():
-                        send_edge(k, side)
+
+            for side in range(2):
+                send_edge(k, side)
 
         for p in range(1, 7):
             quad(p)

time: 50.7 us -> 50.9 us (level)
  no operation moved by 1% of the time
where the time goes in v6:
time: 50.9 us; the launch traced here: 50.8 us
  Pallas kernels  49.5 us (97%)
  local copies, waits for them, and re-layouts  1.32 us (3%)
    pallas_call x1, Pallas kernels, shards(): pl.pallas_call(functools.partial(kernel, regions), out_shape=jax.ShapeDty...  49.5 us
    unnamed x1, local copies, waits for them, and re-layouts  1.32 us

profile of v6, /device:TPU:6, one launch (start us, length us, event | category | flops | bytes accessed | tf_op | source)
XLA Modules:
  0.0 50.8 jit_solution(5475067109924877764)
XLA Ops:
  0.0 49.5 %smoother.1 = bf16[2,8,512,128]{3,2,1,0:T(8,128)(2,1)S(1)} custom-call(bf16[2,8,512,128]{3,2,1,0:T(8,128)(2,1)} %x_hbm.1, f32[2,8,1024]{2,1,0:T(8,128)} %obs_hbm.1, bf16[1024,512]{1,0:T(8,128)(2,1)} %op_hbm.1, f32[8,128]{1,0:T(8,128)} %bitcast.1, s32[2,1024]{1,0:T(2,128)} %mask_hbm.1), custom_call_target="tpu_custom_call" | custom-call | tf_op jit(solution)/shard_map/smoother/pallas_call | solution.py:417
  49.5 1.3 %copy.7 = bf16[2,8,512,128]{3,2,1,0:T(8,128)(2,1)} copy(bf16[2,8,512,128]{3,2,1,0:T(8,128)(2,1)S(1)} %smoother.1) | data formatting | bytes 4194304
